TPU v7x, 256 devices: a whole 4x4x8 slice. The times are simulated.
256 devices in a mesh: pipe: 8 (over x, core), dp: 8 (over z), tensor: 4 (over y).
Axes of the slice: x: 4, y: 4, z: 8, core: 2. Of those that a mesh axis runs over, the one named last changes fastest.
Arguments:
- acts_in: bfloat16 [2, 1024, 4096], P(None, 'dp', 'tensor'), may hold values from -6 to 6
- weights: bfloat16 [8, 4096, 4096], P('pipe', None, 'tensor'), may hold values from -0.046875 to 0.046875
- cotangent: bfloat16 [2, 1024, 4096], P(None, 'dp', 'tensor'), may hold values from -6 to 6
- hist_act: float32 [8, 16], P('pipe'), may hold values from 2 to 12
- hist_weight: float32 [8, 16], P('pipe'), may hold values from 0.01 to 0.1
- hist_grad: float32 [8, 16], P('pipe'), may hold values from 2 to 12
Outputs:
- section_acts: bfloat16 [8, 2, 1024, 4096], P('pipe', None, 'dp', 'tensor')
- section_grads: bfloat16 [8, 2, 1024, 4096], P('pipe', None, 'dp', 'tensor')
- weight_grad: bfloat16 [8, 4096, 4096], P('pipe', 'dp', 'tensor')
- new_hist_act: float32 [8, 16], P('pipe')
- new_hist_weight: float32 [8, 16], P('pipe')
- new_hist_grad: float32 [8, 16], P('pipe')
All inputs are finite; a program needn't handle non-finite values.
Results may differ from a plain program's by a relative error of at most 0.025.
Values may be sent and summed in bfloat16 or wider, within the bound.
A program may use at most 128 MiB of HBM per device.

v0:
```python
import jax
import jax.numpy as jnp
from jax import lax
from jax.sharding import PartitionSpec as P


def copy_for_each(array, axis):
    copies = jnp.broadcast_to(array, (lax.axis_size(axis), *array.shape))
    return lax.all_to_all(copies, axis, split_axis=0, concat_axis=0, tiled=True)


def laid_out(parts, dim):
    parts = jnp.moveaxis(parts, 0, dim)
    dims = parts.shape
    return parts.reshape(*dims[:dim], dims[dim] * dims[dim + 1], *dims[dim + 2 :])


def gathered_copies(array, axis, dim):
    parts = copy_for_each(array, axis)
    return laid_out(parts, dim)


def shifted(value, axis, steps):
    count = lax.axis_size(axis)
    initial, last = (max(0, -steps), min(count, count - steps))
    return lax.ppermute(value, axis, [(source, source + steps) for source in range(initial, last)])


def split_up(array, dim, length):
    before, after = (array.shape[:dim], array.shape[dim + 1 :])
    return jnp.moveaxis(array.reshape(*before, length, -1, *after), dim, 0)


def summed_on_arrival(array, axis, dim):
    parts = split_up(array, dim, lax.axis_size(axis))
    arrived = lax.all_to_all(parts, axis, split_axis=0, concat_axis=0, tiled=True)
    return arrived.astype(jnp.float32).sum(axis=0)


def taken_together(array, axis):
    return copy_for_each(array, axis).max(axis=0)


def in_one(arrays, axis):
    ends = [0]
    for a in arrays:
        ends.append(ends[-1] + a.size)
    so_far = taken_together(jnp.concatenate([a.ravel() for a in arrays]), axis)
    return tuple((so_far[b:e].reshape(a.shape) for a, b, e in zip(arrays, ends, ends[1:])))


def quantize(values, factor, limit_value):
    return jnp.clip(values.astype(jnp.float32) * factor, -limit_value, limit_value).astype(
        jnp.bfloat16
    )


def roll_history(history, newest):
    return jnp.concatenate([jnp.reshape(newest, (1, 1)), history[:, :-1]], axis=1)


def place_row(buffer, slot_index, is_live, new_row):
    old_row = lax.dynamic_index_in_dim(buffer, slot_index, 0, keepdims=False)
    return lax.dynamic_update_index_in_dim(
        buffer, jnp.where(is_live, new_row, old_row), slot_index, 0
    )


def shards(acts_in, weights, cotangent, hist_act, hist_weight, hist_grad):
    section_index = lax.axis_index("pipe")
    section_count = lax.axis_size("pipe")
    micro_count = acts_in.shape[0]
    row_count = acts_in.shape[1]
    own_width = acts_in.shape[2]
    weight = weights[0]
    full_width = weight.shape[0]
    tick_count = micro_count + section_count - 1
    act_factor = 448.0 / jnp.max(hist_act)
    weight_factor = 448.0 / jnp.max(hist_weight)
    grad_factor = 57344.0 / jnp.max(hist_grad)
    forward_factor = 1.0 / (act_factor * weight_factor)
    backward_factor = 1.0 / (grad_factor * weight_factor)
    update_factor = 1.0 / (act_factor * grad_factor)
    quant_weight = quantize(weight, weight_factor, 448.0)
    weight_peak = jnp.max(jnp.abs(weight.astype(jnp.float32)))

    def forward_tick(tick_index, loop_state):
        incoming, outputs, stash, act_peak = loop_state
        micro_index = tick_index - section_index
        is_live = (micro_index >= 0) & (micro_index < micro_count)
        slot_index = jnp.clip(micro_index, 0, micro_count - 1)
        first_input = lax.dynamic_index_in_dim(acts_in, slot_index, 0, keepdims=False)
        section_input = jnp.where(section_index == 0, first_input, incoming)
        quant_local = quantize(section_input, act_factor, 448.0)
        quant_full = gathered_copies(quant_local, "tensor", 1)
        mixed_terms = lax.cond(
            is_live,
            lambda operand: jnp.dot(operand, quant_weight, preferred_element_type=jnp.float32)
            * forward_factor,
            lambda operand: jnp.zeros((row_count, own_width), jnp.float32),
            quant_full,
        )
        section_output = (section_input.astype(jnp.float32) + mixed_terms).astype(jnp.bfloat16)
        outputs = place_row(outputs, slot_index, is_live, section_output)
        stash = place_row(stash, slot_index, is_live, quant_full)
        tick_peak = jnp.where(
            is_live, jnp.max(jnp.abs(section_input.astype(jnp.float32))), jnp.float32(0.0)
        )
        act_peak = jnp.maximum(act_peak, tick_peak)
        incoming = shifted(section_output, "pipe", 1)
        return (incoming, outputs, stash, act_peak)

    forward_init = (
        jnp.zeros((row_count, own_width), jnp.bfloat16),
        jnp.zeros((micro_count, row_count, own_width), jnp.bfloat16),
        jnp.zeros((micro_count, row_count, full_width), jnp.bfloat16),
        jnp.float32(0.0),
    )
    unused, outputs, stash, act_peak = lax.fori_loop(0, tick_count, forward_tick, forward_init)

    def backward_tick(tick_index, loop_state):
        incoming, grads_out, held, grad_peak = loop_state
        micro_index = tick_index - (section_count - 1 - section_index)
        is_live = (micro_index >= 0) & (micro_index < micro_count)
        slot_index = jnp.clip(micro_index, 0, micro_count - 1)
        last_weights = lax.dynamic_index_in_dim(cotangent, slot_index, 0, keepdims=False)
        last_output = lax.dynamic_index_in_dim(outputs, slot_index, 0, keepdims=False)
        last_input = (last_weights.astype(jnp.float32) * last_output.astype(jnp.float32)).astype(
            jnp.bfloat16
        )
        grad_input = jnp.where(section_index == section_count - 1, last_input, incoming)
        quant_grad = quantize(grad_input, grad_factor, 57344.0)
        partial_terms = lax.cond(
            is_live,
            lambda operand: lax.dot_general(
                operand, quant_weight, (((1,), (1,)), ((), ())), preferred_element_type=jnp.float32
            )
            * backward_factor,
            lambda operand: jnp.zeros((row_count, full_width), jnp.float32),
            quant_grad,
        )
        back_terms = summed_on_arrival(partial_terms.astype(jnp.bfloat16), "tensor", 1)
        grad_output = (grad_input.astype(jnp.float32) + back_terms).astype(jnp.bfloat16)
        grads_out = place_row(grads_out, slot_index, is_live, grad_output)
        held = place_row(held, slot_index, is_live, quant_grad)
        tick_peak = jnp.where(
            is_live, jnp.max(jnp.abs(grad_input.astype(jnp.float32))), jnp.float32(0.0)
        )
        grad_peak = jnp.maximum(grad_peak, tick_peak)
        incoming = shifted(grad_output, "pipe", -1)
        return (incoming, grads_out, held, grad_peak)

    held_init = jnp.zeros((micro_count, row_count, own_width), jnp.bfloat16)
    backward_init = (
        jnp.zeros((row_count, own_width), jnp.bfloat16),
        jnp.zeros((micro_count, row_count, own_width), jnp.bfloat16),
        held_init,
        jnp.float32(0.0),
    )
    unused, grads_out, held, grad_peak = lax.fori_loop(0, tick_count, backward_tick, backward_init)
    flat_acts = stash.reshape(-1, full_width)
    flat_grads = held.reshape(-1, own_width)
    weight_sums = lax.psum_scatter(
        (
            lax.dot_general(
                flat_acts, flat_grads, (((0,), (0,)), ((), ())), preferred_element_type=jnp.float32
            )
            * update_factor
        ).astype(jnp.bfloat16),
        "dp",
        scatter_dimension=0,
        tiled=True,
    )
    act_peak, weight_peak, grad_peak = in_one((act_peak, weight_peak, grad_peak), ("dp", "tensor"))
    return (
        outputs[None],
        grads_out[None],
        weight_sums[None],
        roll_history(hist_act, act_peak),
        roll_history(hist_weight, weight_peak),
        roll_history(hist_grad, grad_peak),
    )


def solution(mesh):
    placed = (
        P(None, "dp", "tensor"),
        P("pipe", None, "tensor"),
        P(None, "dp", "tensor"),
        P("pipe", None),
        P("pipe", None),
        P("pipe", None),
    )
    return jax.shard_map(
        shards,
        mesh=mesh,
        in_specs=placed,
        out_specs=(
            P("pipe", None, "dp", "tensor"),
            P("pipe", None, "dp", "tensor"),
            P("pipe", "dp", "tensor"),
            P("pipe", None),
            P("pipe", None),
            P("pipe", None),
        ),
        check_vma=False,
    )
```

profile of v0, /device:TPU:32, one launch (start us, length us, event | category | flops | bytes accessed | tf_op | source)
XLA Modules:
  0.0 697.0 jit_solution(9057805085259018376)
XLA Ops:
  13.1 10.5 %fusion.13 = (f32[]{:T(128)}, bf16[4096,1024]{1,0:T(8,128)(2,1)}) fusion(bf16[1,4096,1024]{2,1,0:T(8,128)(2,1)} %param.15, f32[]{:T(128)S(6)} %div.19), kind=kLoop, calls=%fused_computation.36 | loop fusion | flops 25165824 | bytes 16777224 | tf_op jit(solution)/shard_map/reduce_max | solution.py:85
  25.4 259.0 %while.41 = (s32[]{:T(128)}, bf16[128,1024]{1,0:T(8,128)(2,1)S(1)}, bf16[2,128,1024]{2,1,0:T(8,128)(2,1)S(1)}, bf16[2,128,4096]{1,2,0:T(8,128)(2,1)}, f32[]{:T(1...) while((s32[]{:T(128)}, bf16[128,1024]{1,0:T(8,128)(2,1)S(1)}, ...), condition=%wide.region_6.7_spmd, body=%wide.region_2.6_spmd.sunk | while | flops 1075970048 | bytes 24117608 | solution.py:119
  33.5 14.5 %all-to-all-done = bf16[4,128,1024]{2,1,0:T(8,128)(2,1)S(1)} async-done(((bf16[4,128,1024]{2,1,0:T(8,128)(2,1)}), bf16[4,128,1024]{2,1,0:T(8,128)(2,1)S(1)}, u32[]{:S(2)}, u32[]{:S(2)}) %all-to-all-start) | async-done | bytes 1048608 | tf_op jit(solution)/shard_map/while/body/eval_jaxpr/all_to_all | solution.py:9
  64.3 13.8 %all-to-all-done = bf16[4,128,1024]{2,1,0:T(8,128)(2,1)S(1)} async-done(((bf16[4,128,1024]{2,1,0:T(8,128)(2,1)}), bf16[4,128,1024]{2,1,0:T(8,128)(2,1)S(1)}, u32[]{:S(2)}, u32[]{:S(2)}) %all-to-all-start) | async-done | bytes 1048608 | tf_op jit(solution)/shard_map/while/body/eval_jaxpr/all_to_all | solution.py:9
  94.3 14.4 %all-to-all-done = bf16[4,128,1024]{2,1,0:T(8,128)(2,1)S(1)} async-done(((bf16[4,128,1024]{2,1,0:T(8,128)(2,1)}), bf16[4,128,1024]{2,1,0:T(8,128)(2,1)S(1)}, u32[]{:S(2)}, u32[]{:S(2)}) %all-to-all-start) | async-done | bytes 1048608 | tf_op jit(solution)/shard_map/while/body/eval_jaxpr/all_to_all | solution.py:9
  124.2 15.1 %all-to-all-done = bf16[4,128,1024]{2,1,0:T(8,128)(2,1)S(1)} async-done(((bf16[4,128,1024]{2,1,0:T(8,128)(2,1)}), bf16[4,128,1024]{2,1,0:T(8,128)(2,1)S(1)}, u32[]{:S(2)}, u32[]{:S(2)}) %all-to-all-start) | async-done | bytes 1048608 | tf_op jit(solution)/shard_map/while/body/eval_jaxpr/all_to_all | solution.py:9
  152.0 12.2 %all-to-all-done = bf16[4,128,1024]{2,1,0:T(8,128)(2,1)S(1)} async-done(((bf16[4,128,1024]{2,1,0:T(8,128)(2,1)}), bf16[4,128,1024]{2,1,0:T(8,128)(2,1)S(1)}, u32[]{:S(2)}, u32[]{:S(2)}) %all-to-all-start) | async-done | bytes 1048608 | tf_op jit(solution)/shard_map/while/body/eval_jaxpr/all_to_all | solution.py:9
  179.9 14.0 %all-to-all-done = bf16[4,128,1024]{2,1,0:T(8,128)(2,1)S(1)} async-done(((bf16[4,128,1024]{2,1,0:T(8,128)(2,1)}), bf16[4,128,1024]{2,1,0:T(8,128)(2,1)S(1)}, u32[]{:S(2)}, u32[]{:S(2)}) %all-to-all-start) | async-done | bytes 1048608 | tf_op jit(solution)/shard_map/while/body/eval_jaxpr/all_to_all | solution.py:9
  207.8 14.7 %all-to-all-done = bf16[4,128,1024]{2,1,0:T(8,128)(2,1)S(1)} async-done(((bf16[4,128,1024]{2,1,0:T(8,128)(2,1)}), bf16[4,128,1024]{2,1,0:T(8,128)(2,1)S(1)}, u32[]{:S(2)}, u32[]{:S(2)}) %all-to-all-start) | async-done | bytes 1048608 | tf_op jit(solution)/shard_map/while/body/eval_jaxpr/all_to_all | solution.py:9
  235.7 12.2 %all-to-all-done = bf16[4,128,1024]{2,1,0:T(8,128)(2,1)S(1)} async-done(((bf16[4,128,1024]{2,1,0:T(8,128)(2,1)}), bf16[4,128,1024]{2,1,0:T(8,128)(2,1)S(1)}, u32[]{:S(2)}, u32[]{:S(2)}) %all-to-all-start) | async-done | bytes 1048608 | tf_op jit(solution)/shard_map/while/body/eval_jaxpr/all_to_all | solution.py:9
  263.5 13.1 %all-to-all-done = bf16[4,128,1024]{2,1,0:T(8,128)(2,1)S(1)} async-done(((bf16[4,128,1024]{2,1,0:T(8,128)(2,1)}), bf16[4,128,1024]{2,1,0:T(8,128)(2,1)S(1)}, u32[]{:S(2)}, u32[]{:S(2)}) %all-to-all-start) | async-done | bytes 1048608 | tf_op jit(solution)/shard_map/while/body/eval_jaxpr/all_to_all | solution.py:9
  286.3 303.0 %while.42 = (s32[]{:T(128)}, bf16[128,1024]{1,0:T(8,128)(2,1)S(1)}, bf16[2,128,1024]{2,1,0:T(8,128)(2,1)}, bf16[2,128,1024]{2,1,0:T(8,128)(2,1)}, f32[]{:T(128)}...) while((s32[]{:T(128)}, bf16[128,1024]{1,0:T(8,128)(2,1)S(1)}, ...), condition=%wide.region_13.14_spmd, body=%wide.region_8.13_spmd.sunk | while | flops 1077936128 | bytes 24380272 | solution.py:160
  296.4 14.4 %all-to-all-done.1 = bf16[4,128,1024]{2,1,0:T(8,128)(2,1)S(1)} async-done(((bf16[4,128,1024]{2,1,0:T(8,128)(2,1)}), bf16[4,128,1024]{2,1,0:T(8,128)(2,1)S(1)}, u32[]{:S(2)}, u32[]{:S(2)}) %all-to-all-start.1) | async-done | bytes 1048608 | tf_op jit(solution)/shard_map/while/body/eval_jaxpr/all_to_all | solution.py:36
  325.8 9.9 %all-to-all-done.1 = bf16[4,128,1024]{2,1,0:T(8,128)(2,1)S(1)} async-done(((bf16[4,128,1024]{2,1,0:T(8,128)(2,1)}), bf16[4,128,1024]{2,1,0:T(8,128)(2,1)S(1)}, u32[]{:S(2)}, u32[]{:S(2)}) %all-to-all-start.1) | async-done | bytes 1048608 | tf_op jit(solution)/shard_map/while/body/eval_jaxpr/all_to_all | solution.py:36
  355.3 9.9 %all-to-all-done.1 = bf16[4,128,1024]{2,1,0:T(8,128)(2,1)S(1)} async-done(((bf16[4,128,1024]{2,1,0:T(8,128)(2,1)}), bf16[4,128,1024]{2,1,0:T(8,128)(2,1)S(1)}, u32[]{:S(2)}, u32[]{:S(2)}) %all-to-all-start.1) | async-done | bytes 1048608 | tf_op jit(solution)/shard_map/while/body/eval_jaxpr/all_to_all | solution.py:36
  387.7 9.9 %all-to-all-done.1 = bf16[4,128,1024]{2,1,0:T(8,128)(2,1)S(1)} async-done(((bf16[4,128,1024]{2,1,0:T(8,128)(2,1)}), bf16[4,128,1024]{2,1,0:T(8,128)(2,1)S(1)}, u32[]{:S(2)}, u32[]{:S(2)}) %all-to-all-start.1) | async-done | bytes 1048608 | tf_op jit(solution)/shard_map/while/body/eval_jaxpr/all_to_all | solution.py:36
  419.1 9.9 %all-to-all-done.1 = bf16[4,128,1024]{2,1,0:T(8,128)(2,1)S(1)} async-done(((bf16[4,128,1024]{2,1,0:T(8,128)(2,1)}), bf16[4,128,1024]{2,1,0:T(8,128)(2,1)S(1)}, u32[]{:S(2)}, u32[]{:S(2)}) %all-to-all-start.1) | async-done | bytes 1048608 | tf_op jit(solution)/shard_map/while/body/eval_jaxpr/all_to_all | solution.py:36
  449.7 11.7 %all-to-all-done.1 = bf16[4,128,1024]{2,1,0:T(8,128)(2,1)S(1)} async-done(((bf16[4,128,1024]{2,1,0:T(8,128)(2,1)}), bf16[4,128,1024]{2,1,0:T(8,128)(2,1)S(1)}, u32[]{:S(2)}, u32[]{:S(2)}) %all-to-all-start.1) | async-done | bytes 1048608 | tf_op jit(solution)/shard_map/while/body/eval_jaxpr/all_to_all | solution.py:36
  479.1 9.9 %all-to-all-done.1 = bf16[4,128,1024]{2,1,0:T(8,128)(2,1)S(1)} async-done(((bf16[4,128,1024]{2,1,0:T(8,128)(2,1)}), bf16[4,128,1024]{2,1,0:T(8,128)(2,1)S(1)}, u32[]{:S(2)}, u32[]{:S(2)}) %all-to-all-start.1) | async-done | bytes 1048608 | tf_op jit(solution)/shard_map/while/body/eval_jaxpr/all_to_all | solution.py:36
  491.8 23.7 %collective-permute-done.1 = bf16[128,1024]{1,0:T(8,128)(2,1)S(1)} collective-permute-done((bf16[128,1024]{1,0:T(8,128)(2,1)S(1)}, bf16[128,1024]{1,0:T(8,128)(2,1)S(1)}, u32[]{:S(2)}, u32[]{:S(2)}) %collective-permute-start.1) | collective-permute-done | bytes 262176 | tf_op jit(solution)/shard_map/while/body/eval_jaxpr/ppermute | solution.py:26
  544.5 10.9 %collective-permute-done.1 = bf16[128,1024]{1,0:T(8,128)(2,1)S(1)} collective-permute-done((bf16[128,1024]{1,0:T(8,128)(2,1)S(1)}, bf16[128,1024]{1,0:T(8,128)(2,1)S(1)}, u32[]{:S(2)}, u32[]{:S(2)}) %collective-permute-start.1) | collective-permute-done | bytes 262176 | tf_op jit(solution)/shard_map/while/body/eval_jaxpr/ppermute | solution.py:26
  571.7 13.1 %all-to-all-done.1 = bf16[4,128,1024]{2,1,0:T(8,128)(2,1)S(1)} async-done(((bf16[4,128,1024]{2,1,0:T(8,128)(2,1)}), bf16[4,128,1024]{2,1,0:T(8,128)(2,1)S(1)}, u32[]{:S(2)}, u32[]{:S(2)}) %all-to-all-start.1) | async-done | bytes 1048608 | tf_op jit(solution)/shard_map/while/body/eval_jaxpr/all_to_all | solution.py:36
  597.5 17.9 %all_to_all.29 = f32[32,1,3]{2,1,0:T(1,128)S(1)} all-to-all(f32[32,1,3]{2,1,0:T(1,128)S(1)} %broadcast_in_dim.58), channel_id=1, replica_groups=mesh['pipe'=8,'dp'=8,'tensor'=4] {'dp','tensor'}, dimensions={0} | all-to-all | bytes 768 | tf_op jit(solution)/shard_map/all_to_all | solution.py:9
  619.0 71.1 %reduce-scatter.2.cloned.1.call-done = bf16[512,1024]{1,0:T(8,128)(2,1)} async-done(((bf16[4096,1024]{1,0:T(8,128)(2,1)}), bf16[512,1024]{1,0:T(8,128)(2,1)}) %reduce-scatter.2.cloned.1.call-update) | async-done | bytes 1048592 | tf_op jit(solution)/shard_map/reduce_scatter | solution.py:163
  (250 shorter events, 345.5 us)
Async XLA Ops:
  7.2 682.9 %reduce-scatter.2.cloned.1.call-start = ((), (), s32[]{:S(2)}) async-start(), calls=%async_computation.4 | async-start | bytes 9437184 | tf_op jit(solution)/shard_map/reduce_scatter | solution.py:163
  28.4 19.6 %all-to-all-start = ((bf16[4,128,1024]{2,1,0:T(8,128)(2,1)}), bf16[4,128,1024]{2,1,0:T(8,128)(2,1)S(1)}, u32[]{:S(2)}, u32[]{:S(2)}) async-start(bf16[4,128,1024]{2,1,0:T(8,128)(2,1)} %broadcast_in_dim.60), calls=%async_computation | async-start | bytes 2097152 | tf_op jit(solution)/shard_map/while/body/eval_jaxpr/all_to_all | solution.py:9
  60.2 18.0 %all-to-all-start = ((bf16[4,128,1024]{2,1,0:T(8,128)(2,1)}), bf16[4,128,1024]{2,1,0:T(8,128)(2,1)S(1)}, u32[]{:S(2)}, u32[]{:S(2)}) async-start(bf16[4,128,1024]{2,1,0:T(8,128)(2,1)} %broadcast_in_dim.60), calls=%async_computation | async-start | bytes 2097152 | tf_op jit(solution)/shard_map/while/body/eval_jaxpr/all_to_all | solution.py:9
  90.2 18.5 %all-to-all-start = ((bf16[4,128,1024]{2,1,0:T(8,128)(2,1)}), bf16[4,128,1024]{2,1,0:T(8,128)(2,1)S(1)}, u32[]{:S(2)}, u32[]{:S(2)}) async-start(bf16[4,128,1024]{2,1,0:T(8,128)(2,1)} %broadcast_in_dim.60), calls=%async_computation | async-start | bytes 2097152 | tf_op jit(solution)/shard_map/while/body/eval_jaxpr/all_to_all | solution.py:9
  120.0 19.2 %all-to-all-start = ((bf16[4,128,1024]{2,1,0:T(8,128)(2,1)}), bf16[4,128,1024]{2,1,0:T(8,128)(2,1)S(1)}, u32[]{:S(2)}, u32[]{:S(2)}) async-start(bf16[4,128,1024]{2,1,0:T(8,128)(2,1)} %broadcast_in_dim.60), calls=%async_computation | async-start | bytes 2097152 | tf_op jit(solution)/shard_map/while/body/eval_jaxpr/all_to_all | solution.py:9
  147.9 16.3 %all-to-all-start = ((bf16[4,128,1024]{2,1,0:T(8,128)(2,1)}), bf16[4,128,1024]{2,1,0:T(8,128)(2,1)S(1)}, u32[]{:S(2)}, u32[]{:S(2)}) async-start(bf16[4,128,1024]{2,1,0:T(8,128)(2,1)} %broadcast_in_dim.60), calls=%async_computation | async-start | bytes 2097152 | tf_op jit(solution)/shard_map/while/body/eval_jaxpr/all_to_all | solution.py:9
  175.8 18.1 %all-to-all-start = ((bf16[4,128,1024]{2,1,0:T(8,128)(2,1)}), bf16[4,128,1024]{2,1,0:T(8,128)(2,1)S(1)}, u32[]{:S(2)}, u32[]{:S(2)}) async-start(bf16[4,128,1024]{2,1,0:T(8,128)(2,1)} %broadcast_in_dim.60), calls=%async_computation | async-start | bytes 2097152 | tf_op jit(solution)/shard_map/while/body/eval_jaxpr/all_to_all | solution.py:9
  203.7 18.8 %all-to-all-start = ((bf16[4,128,1024]{2,1,0:T(8,128)(2,1)}), bf16[4,128,1024]{2,1,0:T(8,128)(2,1)S(1)}, u32[]{:S(2)}, u32[]{:S(2)}) async-start(bf16[4,128,1024]{2,1,0:T(8,128)(2,1)} %broadcast_in_dim.60), calls=%async_computation | async-start | bytes 2097152 | tf_op jit(solution)/shard_map/while/body/eval_jaxpr/all_to_all | solution.py:9
  231.5 16.4 %all-to-all-start = ((bf16[4,128,1024]{2,1,0:T(8,128)(2,1)}), bf16[4,128,1024]{2,1,0:T(8,128)(2,1)S(1)}, u32[]{:S(2)}, u32[]{:S(2)}) async-start(bf16[4,128,1024]{2,1,0:T(8,128)(2,1)} %broadcast_in_dim.60), calls=%async_computation | async-start | bytes 2097152 | tf_op jit(solution)/shard_map/while/body/eval_jaxpr/all_to_all | solution.py:9
  259.4 17.2 %all-to-all-start = ((bf16[4,128,1024]{2,1,0:T(8,128)(2,1)}), bf16[4,128,1024]{2,1,0:T(8,128)(2,1)S(1)}, u32[]{:S(2)}, u32[]{:S(2)}) async-start(bf16[4,128,1024]{2,1,0:T(8,128)(2,1)} %broadcast_in_dim.60), calls=%async_computation | async-start | bytes 2097152 | tf_op jit(solution)/shard_map/while/body/eval_jaxpr/all_to_all | solution.py:9
  291.9 18.9 %all-to-all-start.1 = ((bf16[4,128,1024]{2,1,0:T(8,128)(2,1)}), bf16[4,128,1024]{2,1,0:T(8,128)(2,1)S(1)}, u32[]{:S(2)}, u32[]{:S(2)}) async-start(bf16[4,128,1024]{2,1,0:T(8,128)(2,1)} %copy.43), calls=%async_computation.1 | async-start | bytes 2097152 | tf_op jit(solution)/shard_map/while/body/eval_jaxpr/all_to_all | solution.py:36
  321.3 14.4 %all-to-all-start.1 = ((bf16[4,128,1024]{2,1,0:T(8,128)(2,1)}), bf16[4,128,1024]{2,1,0:T(8,128)(2,1)S(1)}, u32[]{:S(2)}, u32[]{:S(2)}) async-start(bf16[4,128,1024]{2,1,0:T(8,128)(2,1)} %copy.43), calls=%async_computation.1 | async-start | bytes 2097152 | tf_op jit(solution)/shard_map/while/body/eval_jaxpr/all_to_all | solution.py:36
  350.8 14.4 %all-to-all-start.1 = ((bf16[4,128,1024]{2,1,0:T(8,128)(2,1)}), bf16[4,128,1024]{2,1,0:T(8,128)(2,1)S(1)}, u32[]{:S(2)}, u32[]{:S(2)}) async-start(bf16[4,128,1024]{2,1,0:T(8,128)(2,1)} %copy.43), calls=%async_computation.1 | async-start | bytes 2097152 | tf_op jit(solution)/shard_map/while/body/eval_jaxpr/all_to_all | solution.py:36
  366.2 11.4 %collective-permute-start.1 = (bf16[128,1024]{1,0:T(8,128)(2,1)S(1)}, bf16[128,1024]{1,0:T(8,128)(2,1)S(1)}, u32[]{:S(2)}, u32[]{:S(2)}) collective-permute-start(bf16[128,1024]{1,0:T(8,128)(2,1)S(1)} %get-tuple-element.759), channel_id=1, source_target_pairs={{32,0},{64,32},{96,64},{128,96},{160,128},{192,160},{224,192},{33,... | collective-permute-start | bytes 786440 | tf_op jit(solution)/shard_map/while/body/eval_jaxpr/ppermute | solution.py:26
  383.2 14.4 %all-to-all-start.1 = ((bf16[4,128,1024]{2,1,0:T(8,128)(2,1)}), bf16[4,128,1024]{2,1,0:T(8,128)(2,1)S(1)}, u32[]{:S(2)}, u32[]{:S(2)}) async-start(bf16[4,128,1024]{2,1,0:T(8,128)(2,1)} %copy.43), calls=%async_computation.1 | async-start | bytes 2097152 | tf_op jit(solution)/shard_map/while/body/eval_jaxpr/all_to_all | solution.py:36
  398.6 10.4 %collective-permute-start.1 = (bf16[128,1024]{1,0:T(8,128)(2,1)S(1)}, bf16[128,1024]{1,0:T(8,128)(2,1)S(1)}, u32[]{:S(2)}, u32[]{:S(2)}) collective-permute-start(bf16[128,1024]{1,0:T(8,128)(2,1)S(1)} %get-tuple-element.759), channel_id=1, source_target_pairs={{32,0},{64,32},{96,64},{128,96},{160,128},{192,160},{224,192},{33,... | collective-permute-start | bytes 786440 | tf_op jit(solution)/shard_map/while/body/eval_jaxpr/ppermute | solution.py:26
  414.6 14.4 %all-to-all-start.1 = ((bf16[4,128,1024]{2,1,0:T(8,128)(2,1)}), bf16[4,128,1024]{2,1,0:T(8,128)(2,1)S(1)}, u32[]{:S(2)}, u32[]{:S(2)}) async-start(bf16[4,128,1024]{2,1,0:T(8,128)(2,1)} %copy.43), calls=%async_computation.1 | async-start | bytes 2097152 | tf_op jit(solution)/shard_map/while/body/eval_jaxpr/all_to_all | solution.py:36
  430.0 9.6 %collective-permute-start.1 = (bf16[128,1024]{1,0:T(8,128)(2,1)S(1)}, bf16[128,1024]{1,0:T(8,128)(2,1)S(1)}, u32[]{:S(2)}, u32[]{:S(2)}) collective-permute-start(bf16[128,1024]{1,0:T(8,128)(2,1)S(1)} %get-tuple-element.759), channel_id=1, source_target_pairs={{32,0},{64,32},{96,64},{128,96},{160,128},{192,160},{224,192},{33,... | collective-permute-start | bytes 786440 | tf_op jit(solution)/shard_map/while/body/eval_jaxpr/ppermute | solution.py:26
  445.2 16.2 %all-to-all-start.1 = ((bf16[4,128,1024]{2,1,0:T(8,128)(2,1)}), bf16[4,128,1024]{2,1,0:T(8,128)(2,1)S(1)}, u32[]{:S(2)}, u32[]{:S(2)}) async-start(bf16[4,128,1024]{2,1,0:T(8,128)(2,1)} %copy.43), calls=%async_computation.1 | async-start | bytes 2097152 | tf_op jit(solution)/shard_map/while/body/eval_jaxpr/all_to_all | solution.py:36
  474.5 14.4 %all-to-all-start.1 = ((bf16[4,128,1024]{2,1,0:T(8,128)(2,1)}), bf16[4,128,1024]{2,1,0:T(8,128)(2,1)S(1)}, u32[]{:S(2)}, u32[]{:S(2)}) async-start(bf16[4,128,1024]{2,1,0:T(8,128)(2,1)} %copy.43), calls=%async_computation.1 | async-start | bytes 2097152 | tf_op jit(solution)/shard_map/while/body/eval_jaxpr/all_to_all | solution.py:36
  490.0 25.5 %collective-permute-start.1 = (bf16[128,1024]{1,0:T(8,128)(2,1)S(1)}, bf16[128,1024]{1,0:T(8,128)(2,1)S(1)}, u32[]{:S(2)}, u32[]{:S(2)}) collective-permute-start(bf16[128,1024]{1,0:T(8,128)(2,1)S(1)} %get-tuple-element.759), channel_id=1, source_target_pairs={{32,0},{64,32},{96,64},{128,96},{160,128},{192,160},{224,192},{33,... | collective-permute-start | bytes 786440 | tf_op jit(solution)/shard_map/while/body/eval_jaxpr/ppermute | solution.py:26
  527.3 14.4 %all-to-all-start.1 = ((bf16[4,128,1024]{2,1,0:T(8,128)(2,1)}), bf16[4,128,1024]{2,1,0:T(8,128)(2,1)S(1)}, u32[]{:S(2)}, u32[]{:S(2)}) async-start(bf16[4,128,1024]{2,1,0:T(8,128)(2,1)} %copy.43), calls=%async_computation.1 | async-start | bytes 2097152 | tf_op jit(solution)/shard_map/while/body/eval_jaxpr/all_to_all | solution.py:36
  542.7 12.7 %collective-permute-start.1 = (bf16[128,1024]{1,0:T(8,128)(2,1)S(1)}, bf16[128,1024]{1,0:T(8,128)(2,1)S(1)}, u32[]{:S(2)}, u32[]{:S(2)}) collective-permute-start(bf16[128,1024]{1,0:T(8,128)(2,1)S(1)} %get-tuple-element.759), channel_id=1, source_target_pairs={{32,0},{64,32},{96,64},{128,96},{160,128},{192,160},{224,192},{33,... | collective-permute-start | bytes 786440 | tf_op jit(solution)/shard_map/while/body/eval_jaxpr/ppermute | solution.py:26
  567.2 17.6 %all-to-all-start.1 = ((bf16[4,128,1024]{2,1,0:T(8,128)(2,1)}), bf16[4,128,1024]{2,1,0:T(8,128)(2,1)S(1)}, u32[]{:S(2)}, u32[]{:S(2)}) async-start(bf16[4,128,1024]{2,1,0:T(8,128)(2,1)} %copy.43), calls=%async_computation.1 | async-start | bytes 2097152 | tf_op jit(solution)/shard_map/while/body/eval_jaxpr/all_to_all | solution.py:36
  (17 other events, 167.2 us)
Sparse Core Ops, SparseCore 0:
  596.9 93.2 reduce-scatter.1
where the time goes:
time: 704 us; the launch traced here: 697 us
  waiting for transfers between devices  369 us (52%)
  starting transfers between devices  108 us (15%)
  other arithmetic  88.7 us (13%)
  local copies, waits for them, and re-layouts  56.3 us (8%)
  matrix products  29.3 us (4%)
  blocking collectives  17.9 us (3%)
  between operations  16.2 us (2%)
  loops' own time  11.7 us (2%)
    all_to_all x9, waiting for transfers between devices, copy_for_each(): return lax.all_to_all(copies, axis, split_axis=0, concat_axis=0, tiled=True)  124 us
    all_to_all x9, waiting for transfers between devices, summed_on_arrival(): lax.all_to_all(parts, axis, split_axis=0, concat_axis=0, tiled=True)  98.5 us
    ppermute x18, waiting for transfers between devices, shifted(): lax.ppermute(value, axis, [(source, source + steps) for source in range(i...  75.3 us
    reduce_scatter x1, waiting for transfers between devices, shards(): lax.psum_scatter((lax.dot_general(flat_acts, flat_grads, (((0,), (0,)), (...  71.1 us
    ppermute x18, starting transfers between devices, shifted(): lax.ppermute(value, axis, [(source, source + steps) for source in range(i...  43.7 us
    dynamic_update_slice x36, other arithmetic, place_row(): lax.dynamic_update_index_in_dim(buffer, jnp.where(is_live, new_row, old_r...  38.8 us
    all_to_all x9, starting transfers between devices, copy_for_each(): return lax.all_to_all(copies, axis, split_axis=0, concat_axis=0, tiled=True)  32.6 us
    all_to_all x9, starting transfers between devices, summed_on_arrival(): lax.all_to_all(parts, axis, split_axis=0, concat_axis=0, tiled=True)  31.7 us
  transfers between devices with their start and end apart: 37, of which 28 were waited for; matrix products, arithmetic and copies ran while one was open for 5% of the time, Pallas kernels for 0%

commit v1 on v0

v1 whole, which is shorter than its diff:
```python
import functools

import jax
import jax.numpy as jnp
from jax import lax
from jax.experimental import pallas as pl
from jax.experimental.pallas import tpu as pltpu
from jax.sharding import PartitionSpec as P

MESH = pl.DeviceIdType.MESH
F32 = jnp.float32
BF16 = jnp.bfloat16
CHUNK = 32


def quantize(values, factor, limit):
    return jnp.clip(values.astype(F32) * factor, -limit, limit).astype(BF16)


def gray(j):
    return j ^ (j >> 1)


def kernel(
    S, Z, T, n, R,
    acts, weights, cot, hist_act, hist_weight, hist_grad,
    out_acts, out_grads, out_wgrad, out_peaks,
    w, xg, xq, ar, gr, outv, gin, gout, gq, ps, pr, pr2, rr, cotv, wg, amax, wmax, gmax, pks, pky, pkm, pkz,
    ld_w, ld_x, ld_c, st_o, st_g, st_w,
    f_recv, fg_send, fo_send, a_send, a_recv, p_send, p_recv, p2_send, p2_recv,
    r_send, r_recv, gi_send, gi_recv, go_send, go_recv, z_send, z_recv,
    ky_send, ky_recv, kz_send, kz_recv,
):
    s = lax.axis_index("pipe")
    z = lax.axis_index("dp")
    y = lax.axis_index("tensor")
    H = Z // T
    C = w.shape[1]
    odd = lax.rem(s, 2)
    even = odd == 0
    is_odd = odd == 1
    first = s == 0
    last = s == S - 1
    pair = s + 1 - 2 * odd
    cross = s - 1 + 2 * odd
    has_cross = (cross >= 0) & (cross < S)

    def at_y(d):
        return lax.rem(y + d, T)

    def at_z(d):
        return lax.rem(z + d, Z)

    def rcopy(src, dst, send, recv, **device):
        return pltpu.make_async_remote_copy(
            src_ref=src, dst_ref=dst, send_sem=send, recv_sem=recv, device_id=device, device_id_type=MESH
        )

    barrier = pltpu.get_barrier_semaphore()
    for d in range(1, T):
        pl.semaphore_signal(barrier, inc=1, device_id={"tensor": at_y(d)}, device_id_type=MESH)
    for d in range(1, Z):
        pl.semaphore_signal(barrier, inc=1, device_id={"dp": at_z(d)}, device_id_type=MESH)
    for d in range(T):
        pl.semaphore_signal(barrier, inc=1, device_id={"pipe": pair, "tensor": at_y(d)}, device_id_type=MESH)

    @pl.when(has_cross)
    def _():
        pl.semaphore_signal(barrier, inc=1, device_id={"pipe": cross}, device_id_type=MESH)

    own = pl.ds(y * H, H)

    def load_w(r):
        return pltpu.make_async_copy(weights.at[r], w.at[r], ld_w.at[r])

    def load_x(c, h):
        return pltpu.make_async_copy(
            acts.at[c, :, pl.ds(h * C, C)], xg.at[c, y * H + h], ld_x.at[c, h]
        )

    load_c = pltpu.make_async_copy(cot, cotv, ld_c)

    @pl.when(first)
    def _():
        for h in range(H):
            lax.fori_loop(0, n, lambda c, u: (load_x(c, h).start(), u)[1], 0)

    lax.fori_loop(0, Z, lambda r, u: (load_w(r).start(), u)[1], 0)

    @pl.when(last)
    def _():
        load_c.start()

    ha = jnp.max(hist_act[...], axis=1, keepdims=True)
    hw = jnp.max(hist_weight[...], axis=1, keepdims=True)
    hg = jnp.max(hist_grad[...], axis=1, keepdims=True)
    act_factor = 448.0 / ha
    weight_factor = 448.0 / hw
    grad_factor = 57344.0 / hg
    forward_factor = 1.0 / (act_factor * weight_factor)
    backward_factor = 1.0 / (grad_factor * weight_factor)
    update_factor = 1.0 / (act_factor * grad_factor)

    amax[...] = jnp.zeros_like(amax)
    wmax[...] = jnp.zeros_like(wmax)
    gmax[...] = jnp.zeros_like(gmax)

    @pl.when(first)
    def _():
        for h in range(H):
            lax.fori_loop(0, n, lambda c, u: (load_x(c, h).wait(), u)[1], 0)

    pl.semaphore_wait(barrier, (T - 1) + (Z - 1) + T + has_cross.astype(jnp.int32))

    def fwd_copy(c, k, send, **device):
        return rcopy(xg.at[c, own], xg.at[c, own], send, f_recv.at[c, k], **device)

    def gather_copy(c, d):
        return fwd_copy(c, y, fg_send.at[c, d - 1], tensor=at_y(d))

    def out_copy(c, d):
        return rcopy(
            outv.at[c], xg.at[c, own], fo_send.at[c, d], f_recv.at[c, y], pipe=pair, tensor=at_y(d)
        )

    def hop_copy(c):
        return rcopy(outv.at[c], xg.at[c, own], fo_send.at[c, 0], f_recv.at[c, y], pipe=cross)

    def wait_block(c, yb):
        blk = xg.at[c, pl.ds(yb * H, H)]
        rcopy(blk, blk, fo_send.at[c, 0], f_recv.at[c, yb], pipe=pair).wait_recv()

    def act_copy(c, d):
        r = at_z(d)
        return rcopy(xq.at[c, r], ar.at[c, z], a_send.at[c, d - 1], a_recv.at[c, z], dp=r)

    @pl.when(first)
    def _():
        def go(c, u):
            for d in (2, 1, 3):
                gather_copy(c, d).start()
            return u
        lax.fori_loop(0, n, go, 0)

    def quant_w(r, u):
        load_w(r).wait()
        raw = w[r].astype(F32)
        wmax[...] = jnp.maximum(wmax[...], jnp.max(jnp.abs(raw), axis=0, keepdims=True))
        w[r] = jnp.clip(raw * weight_factor, -448.0, 448.0).astype(BF16)
        return u

    lax.fori_loop(0, Z, quant_w, 0)

    def store_out(c, h):
        return pltpu.make_async_copy(outv.at[c, h], out_acts.at[c, :, pl.ds(h * C, C)], st_o.at[c, h])

    def forward(c, u):
        @pl.when(jnp.logical_not(first))
        def _():
            wait_block(c, y)

            @pl.when(even)
            def _():
                for d in (2, 1, 3):
                    gather_copy(c, d).start()

        total = jnp.zeros((R, H * C), F32)
        for j in range(T):
            yb = at_y(gray(j))
            if j:
                wait_block(c, yb)
            for h in range(H):
                r = yb * H + h
                x = xg[c, r]
                if j == 0:
                    amax[h] = jnp.maximum(amax[h], jnp.max(jnp.abs(x.astype(F32)), axis=0, keepdims=True))
                q = quantize(x, act_factor, 448.0)
                xq[c, r] = q
                total = total + jnp.dot(q, w[r], preferred_element_type=F32)
        for h in range(H):
            o = xg[c, y * H + h].astype(F32) + total[:, h * C : (h + 1) * C] * forward_factor
            outv[c, h] = o.astype(BF16)

        @pl.when(even)
        def _():
            for d in (2, 1, 3, 0):
                out_copy(c, d).start()

        @pl.when(is_odd & has_cross)
        def _():
            hop_copy(c).start()

        for d in range(1, Z):
            act_copy(c, d).start()
        ar[c, z] = xq[c, z]
        for h in range(H):
            store_out(c, h).start()
        return u

    lax.fori_loop(0, n, forward, 0)

    def part_copy(c, d):
        yb = at_y(d)
        return rcopy(ps.at[c, yb], pr.at[c, y], p_send.at[c, d], p_recv.at[c, y], pipe=pair, tensor=yb)

    def peer_copy(c, d):
        yb = at_y(d)
        return rcopy(ps.at[c, yb], pr2.at[c, y], p2_send.at[c, d - 1], p2_recv.at[c, y], tensor=yb)

    def rest_copy(c):
        return rcopy(gin.at[c], rr.at[c], r_send.at[c], r_recv.at[c], pipe=pair)

    def back_copy(c):
        return rcopy(gin.at[c], gout.at[c], go_send.at[c], go_recv.at[c], pipe=pair)

    def g_hop_copy(c):
        return rcopy(gout.at[c], gin.at[c], gi_send.at[c], gi_recv.at[c], pipe=cross)

    def z_copy(c, d):
        return rcopy(gq.at[c], gr.at[c, z], z_send.at[c, d - 1], z_recv.at[c, z], dp=at_z(d))

    def store_g(c):
        return pltpu.make_async_copy(gout.at[c], out_grads.at[c], st_g.at[c])

    @pl.when(last)
    def _():
        load_c.wait()

    def backward(c, u):
        @pl.when(last)
        def _():
            for h in range(H):
                part = cotv[c, :, h * C : (h + 1) * C].astype(F32) * outv[c, h].astype(F32)
                gin[c, :, h * C : (h + 1) * C] = part.astype(BF16)

        @pl.when(even)
        def _():
            rest_copy(c).wait_recv()
            for k in range(T):
                rcopy(pr.at[c, k], pr.at[c, k], p_send.at[c, 0], p_recv.at[c, k], pipe=pair).wait_recv()
            for h in range(H):
                g = rr[c, :, h * C : (h + 1) * C].astype(F32)
                for k in range(T):
                    g = g + pr[c, k, h].astype(F32)
                gin[c, :, h * C : (h + 1) * C] = g.astype(BF16)
            back_copy(c).start()

        @pl.when(is_odd & has_cross)
        def _():
            g_hop_copy(c).wait_recv()

        g = gin[c]
        gmax[...] = jnp.maximum(gmax[...], jnp.max(jnp.abs(g.astype(F32)), axis=0, keepdims=True))
        q = quantize(g, grad_factor, 57344.0)
        gq[c] = q

        @pl.when(is_odd)
        def _():
            rest_copy(c).start()

        for d in (2, 1, 3, 0):
            yb = at_y(d)
            for h in range(H):
                part = lax.dot_general(
                    q, w[yb * H + h], (((1,), (1,)), ((), ())), preferred_element_type=F32
                )
                ps[c, yb, h] = (part * backward_factor).astype(BF16)

            @pl.when(is_odd)
            def _():
                part_copy(c, d).start()

            if d:
                @pl.when(even)
                def _():
                    peer_copy(c, d).start()

        for d in range(1, Z):
            z_copy(c, d).start()
        gr[c, z] = q

        @pl.when(even)
        def _():
            for d in (3, 1, 2):
                k = at_y(d)
                rcopy(pr2.at[c, k], pr2.at[c, k], p_send.at[c, 0], p2_recv.at[c, k], pipe=pair).wait_recv()
            for h in range(H):
                g = gin[c, :, h * C : (h + 1) * C].astype(F32)
                g = g + ps[c, y, h].astype(F32)
                for d in range(1, T):
                    g = g + pr2[c, at_y(d), h].astype(F32)
                gout[c, :, h * C : (h + 1) * C] = g.astype(BF16)

            @pl.when(has_cross)
            def _():
                g_hop_copy(c).start()
            store_g(c).start()

        return u

    lax.fori_loop(0, n, backward, 0)

    lanes = pks.shape[-1]
    peak_a = jnp.max(jnp.maximum(amax[0], amax[H - 1]), axis=1, keepdims=True)
    peak_w = jnp.max(wmax[...], axis=1, keepdims=True)
    peak_g = jnp.max(gmax[...], axis=1, keepdims=True)
    row = lax.broadcasted_iota(jnp.int32, (8, lanes), 0)
    tile = jnp.where(row == 0, peak_a, jnp.where(row == 1, peak_w, peak_g))
    pks[...] = tile

    def ky_copy(d):
        return rcopy(pks, pky.at[y], ky_send.at[d - 1], ky_recv.at[y], tensor=at_y(d))

    def kz_copy(d):
        return rcopy(pkm, pkz.at[z], kz_send.at[d - 1], kz_recv.at[z], dp=at_z(d))

    for d in range(1, T):
        ky_copy(d).start()
    for d in range(1, T):
        k = at_y(d)
        rcopy(pks, pky.at[k], ky_send.at[0], ky_recv.at[k], tensor=k).wait_recv()
        tile = jnp.maximum(tile, pky[k])
    pkm[...] = tile
    for d in range(1, Z):
        kz_copy(d).start()

    def wait_rows(c, u):
        for d in range(1, Z):
            k = at_z(d)
            rcopy(ar.at[c, k], ar.at[c, k], z_send.at[c, 0], a_recv.at[c, k], dp=k).wait_recv()
            rcopy(gr.at[c, k], gr.at[c, k], z_send.at[c, 0], z_recv.at[c, k], dp=k).wait_recv()
        return u

    lax.fori_loop(0, n, wait_rows, 0)
    left = ar[...].reshape(n * Z * R, C)
    right = gr[...].reshape(n * Z * R, H * C)
    prod = lax.dot_general(left, right, (((0,), (0,)), ((), ())), preferred_element_type=F32)
    wg[...] = (prod * update_factor).astype(BF16)
    st = pltpu.make_async_copy(wg, out_wgrad, st_w)
    st.start()

    for d in range(1, Z):
        k = at_z(d)
        rcopy(pkm, pkz.at[k], kz_send.at[0], kz_recv.at[k], dp=k).wait_recv()
        tile = jnp.maximum(tile, pkz[k])
    out_peaks[...] = tile

    for d in range(1, T):
        ky_copy(d).wait_send()
    for d in range(1, Z):
        kz_copy(d).wait_send()

    def close(c, u):
        @pl.when(even)
        def _():
            for d in range(1, T):
                gather_copy(c, d).wait_send()
                peer_copy(c, d).wait_send()
            for d in range(T):
                out_copy(c, d).wait_send()
            back_copy(c).wait_send()

            @pl.when(has_cross)
            def _():
                g_hop_copy(c).wait_send()

        @pl.when(is_odd)
        def _():
            for d in range(T):
                part_copy(c, d).wait_send()
            rest_copy(c).wait_send()
            back_copy(c).wait_recv()
            store_g(c).start()

            @pl.when(has_cross)
            def _():
                hop_copy(c).wait_send()

        for d in range(1, Z):
            act_copy(c, d).wait_send()
            z_copy(c, d).wait_send()
        for h in range(H):
            store_out(c, h).wait()
        return u

    lax.fori_loop(0, n, close, 0)
    lax.fori_loop(0, n, lambda c, u: (store_g(c).wait(), u)[1], 0)
    st.wait()


def step(acts_in, weights, cotangent, hist_act, hist_weight, hist_grad):
    S, Z, T = (lax.axis_size(a) for a in ("pipe", "dp", "tensor"))
    micro, rows, width = acts_in.shape
    depth = weights.shape[1]
    R = min(CHUNK, rows)
    n = micro * rows // R
    H = Z // T
    C = depth // Z
    acts = acts_in.reshape(n, R, width)
    cot = cotangent.reshape(n, R, width)
    w = weights.reshape(Z, C, width)
    any_ = pl.BlockSpec(memory_space=pl.ANY)
    vmem = pl.BlockSpec(memory_space=pltpu.VMEM)
    dma = pltpu.SemaphoreType.DMA
    b = lambda *shape: pltpu.VMEM(shape, BF16)
    f = lambda *shape: pltpu.VMEM(shape, F32)
    out_acts, out_grads, out_w, peaks = pl.pallas_call(
        functools.partial(kernel, S, Z, T, n, R),
        out_shape=(
            jax.ShapeDtypeStruct((n, R, width), BF16),
            jax.ShapeDtypeStruct((n, R, width), BF16),
            jax.ShapeDtypeStruct((C, width), BF16),
            jax.ShapeDtypeStruct((8, 128), F32),
        ),
        in_specs=[any_, any_, any_, vmem, vmem, vmem],
        out_specs=(any_, any_, any_, vmem),
        scratch_shapes=[
            b(Z, C, width), b(n, Z, R, C), b(n, Z, R, C), b(n, Z, R, C), b(n, Z, R, width),
            b(n, H, R, C), b(n, R, width), b(n, R, width), b(n, R, width),
            b(n, T, H, R, C), b(n, T, H, R, C), b(n, T, H, R, C), b(n, R, width), b(n, R, width),
            b(C, width), f(H, 1, C), f(1, width), f(1, width),
            f(8, 128), f(T, 8, 128), f(8, 128), f(Z, 8, 128),
            dma((Z,)), dma((n, H)), dma, dma((n, H)), dma((n,)), dma,
            dma((n, T)), dma((n, T - 1)), dma((n, T)), dma((n, Z - 1)), dma((n, Z)),
            dma((n, T)), dma((n, T)), dma((n, T - 1)), dma((n, T)),
            dma((n,)), dma((n,)), dma((n,)), dma((n,)), dma((n,)), dma((n,)),
            dma((n, Z - 1)), dma((n, Z)),
            dma((T - 1,)), dma((T,)), dma((Z - 1,)), dma((Z,)),
        ],
        compiler_params=pltpu.CompilerParams(
            collective_id=0, has_side_effects=True, vmem_limit_bytes=60 * 1024 * 1024
        ),
    )(acts, w, cot, hist_act, hist_weight, hist_grad)

    def roll(history, newest):
        return jnp.concatenate([newest, history[:, :-1]], axis=1)

    return (
        out_acts.reshape(1, micro, rows, width),
        out_grads.reshape(1, micro, rows, width),
        out_w[None],
        roll(hist_act, peaks[0:1, 0:1]),
        roll(hist_weight, peaks[1:2, 0:1]),
        roll(hist_grad, peaks[2:3, 0:1]),
    )


def solution(mesh):
    placed = (
        P(None, "dp", "tensor"),
        P("pipe", None, "tensor"),
        P(None, "dp", "tensor"),
        P("pipe", None),
        P("pipe", None),
        P("pipe", None),
    )
    return jax.shard_map(
        step,
        mesh=mesh,
        in_specs=placed,
        out_specs=(
            P("pipe", None, "dp", "tensor"),
            P("pipe", None, "dp", "tensor"),
            P("pipe", "dp", "tensor"),
            P("pipe", None),
            P("pipe", None),
            P("pipe", None),
        ),
        check_vma=False,
    )
```

time: 704 us -> 276 us (0.39)
  waiting for transfers between devices: 369 us -> 0 us
  Pallas kernels: 0 us -> 262 us
  starting transfers between devices: 108 us -> 0 us
  other arithmetic: 88.7 us -> 3.11 us
  local copies, waits for them, and re-layouts: 56.3 us -> 7.33 us
  matrix products: 29.3 us -> 0 us
  blocking collectives: 17.9 us -> 0 us
  between operations: 16.2 us -> 0.67 us
  loops' own time: 11.7 us -> 0 us
    pallas_call x0 -> x1, Pallas kernels: none -> 262 us  [step(): pl.pallas_call(functools.partial(kernel, S, Z, T, n, R), out_shape=(jax.S...]
    all_to_all x18 -> x0, waiting for transfers between devices: 222 us -> none  [the longest x9 124 us: copy_for_each(): return lax.all_to_all(copies, axis, split_axis=0, concat_axis=0, tiled=True)]
    ppermute x18 -> x0, waiting for transfers between devices: 75.3 us -> none  [shifted(): lax.ppermute(value, axis, [(source, source + steps) for source in range(i...]
    reduce_scatter x1 -> x0, waiting for transfers between devices: 71.1 us -> none  [shards(): lax.psum_scatter((lax.dot_general(flat_acts, flat_grads, (((0,), (0,)), (...]
    all_to_all x18 -> x0, starting transfers between devices: 64.3 us -> none  [the longest x9 32.6 us: copy_for_each(): return lax.all_to_all(copies, axis, split_axis=0, concat_axis=0, tiled=True)]
    reduce_max x23 -> x0, other arithmetic: 43.9 us -> none  [the longest x9 15 us: backward_tick(): jnp.max(jnp.abs(grad_input.astype(jnp.float32)))]
    ppermute x18 -> x0, starting transfers between devices: 43.7 us -> none  [shifted(): lax.ppermute(value, axis, [(source, source + steps) for source in range(i...]
    dynamic_update_slice x36 -> x0, other arithmetic: 38.8 us -> none  [place_row(): lax.dynamic_update_index_in_dim(buffer, jnp.where(is_live, new_row, old_r...]
  transfers between devices with their start and end apart: 37 -> 0, of which waited for: 28 -> 0; matrix products, arithmetic and copies ran while one was open for 5% -> 0% of each run, Pallas kernels for 0% -> 0%
where the time goes in v1:
time: 276 us; the launch traced here: 273 us
  Pallas kernels  262 us (95%)
  local copies, waits for them, and re-layouts  7.33 us (3%)
  other arithmetic  3.11 us (1%)
    pallas_call x1, Pallas kernels, step(): pl.pallas_call(functools.partial(kernel, S, Z, T, n, R), out_shape=(jax.S...  262 us
    unnamed x9, local copies, waits for them, and re-layouts  6.01 us

profile of v1, /device:TPU:32, one launch (start us, length us, event | category | flops | bytes accessed | tf_op | source)
XLA Modules:
  0.0 273.4 jit_solution(11409359911660093742)
XLA Ops:
  0.6 0.0 copy-start.2
  0.6 0.0 copy-start.1
  0.7 0.0 copy-start
  0.7 262.3 %shard_map.109 = (bf16[8,32,1024]{2,1,0:T(8,128)(2,1)}, bf16[8,32,1024]{2,1,0:T(8,128)(2,1)}, bf16[512,1024]{1,0:T(8,128)(2,1)}, f32[8,128]{1,0:T(8,128)}) custom-call(bf16[8,32,1024]{2,1,0:T(8,128)(2,1)} %bitcast.11, bf16[8,512,1024]{2,1,0:T(8,128)(2,1)} %bitcast.9, bf16[8,32,1024]{2,1,0:T(8,128)(2,1)} %bitcast.12, f32[1,16]{1,0:T(1,128)} %hist_act.1, ...), custom_call_target="tpu_custom_call" | custom-call | tf_op jit(solution)/shard_map/pallas_call | solution.py:407
  262.9 1.3 fusion
  264.3 0.0 copy-done.2
  264.3 1.2 pad_maximum_fusion.2
  265.5 0.0 copy-done.1
  265.5 0.0 copy-done
  265.5 1.9 pad_maximum_fusion
  267.4 1.9 copy.15
  269.3 1.9 copy.16
  271.1 2.3 copy.17
Async XLA Ops:
  0.6 263.6 %copy-start.2 = (f32[1,16]{1,0:T(1,128)S(1)}, f32[1,16]{1,0:T(1,128)}, u32[]{:S(2)}) copy-start(f32[1,16]{1,0:T(1,128)} %hist_grad.1) | copy-start | bytes 196
  0.6 264.9 %copy-start.1 = (f32[1,16]{1,0:T(1,128)S(1)}, f32[1,16]{1,0:T(1,128)}, u32[]{:S(2)}) copy-start(f32[1,16]{1,0:T(1,128)} %hist_weight.1) | copy-start | bytes 196
  0.7 264.9 %copy-start = (f32[1,16]{1,0:T(1,128)S(1)}, f32[1,16]{1,0:T(1,128)}, u32[]{:S(2)}) copy-start(f32[1,16]{1,0:T(1,128)} %hist_act.1) | copy-start | bytes 196

commit v2 on v1

v2 whole, which is shorter than its diff:
```python
import contextlib
import functools

import jax
import jax.numpy as jnp
from jax import lax
from jax.experimental import pallas as pl
from jax.experimental.pallas import tpu as pltpu
from jax.sharding import PartitionSpec as P

MESH = pl.DeviceIdType.MESH
F32 = jnp.float32
BF16 = jnp.bfloat16
CHUNK = 16
AHEAD = 3
LAG = 4

scope = lambda name: contextlib.nullcontext()


def quantize(values, factor, limit):
    return jnp.clip(values.astype(F32) * factor, -limit, limit).astype(BF16)


def gray(j):
    return j ^ (j >> 1)


def kernel(
    S, Z, T, n, R,
    acts, weights, cot, hist_act, hist_weight, hist_grad,
    out_acts, out_grads, out_wgrad, out_peaks,
    w, wt, xg, xq, ar, gr, outv, gin, gout, gq, ps, pr, pr0, cotv, acc, wg, amax, wmax, gmax, pks, pky, pkm, pkz,
    ld_w, ld_x, ld_c, st_o, st_g, st_w,
    f_recv, fg_send, fo_send, a_send, a_recv, p_send, p_recv, p0_recv, go_send, go_recv, z_send, zf_recv, zo_recv,
    ky_send, ky_recv, kz_send, kz_recv,
):
    s = lax.axis_index("pipe")
    z = lax.axis_index("dp")
    y = lax.axis_index("tensor")
    H = Z // T
    C = w.shape[1]
    odd = lax.rem(s, 2)
    even = odd == 0
    is_odd = odd == 1
    first = s == 0
    last = s == S - 1
    not_last = jnp.logical_not(last)
    not_first = jnp.logical_not(first)
    up = jnp.minimum(s + 1, S - 1)
    down = jnp.maximum(s - 1, 0)

    def at_y(d):
        return lax.rem(y + d, T)

    def at_z(d):
        return lax.rem(z + d, Z)

    def rcopy(src, dst, send, recv, **device):
        return pltpu.make_async_remote_copy(
            src_ref=src, dst_ref=dst, send_sem=send, recv_sem=recv, device_id=device, device_id_type=MESH
        )

    def drain_send(sem, ref):
        rcopy(ref, ref, sem, sem, tensor=at_y(1)).wait_send()

    def drain_recv(sem, ref):
        rcopy(ref, ref, sem, sem, tensor=at_y(1)).wait_recv()

    barrier = pltpu.get_barrier_semaphore()
    for d in range(1, T):
        pl.semaphore_signal(barrier, inc=1, device_id={"tensor": at_y(d)}, device_id_type=MESH)
    for d in range(1, Z):
        pl.semaphore_signal(barrier, inc=1, device_id={"dp": at_z(d)}, device_id_type=MESH)
    for d in range(T):
        @pl.when(not_last)
        def _():
            pl.semaphore_signal(barrier, inc=1, device_id={"pipe": up, "tensor": at_y(d)}, device_id_type=MESH)

        @pl.when(not_first)
        def _():
            pl.semaphore_signal(barrier, inc=1, device_id={"pipe": down, "tensor": at_y(d)}, device_id_type=MESH)

    own = pl.ds(y * H, H)

    def load_w(r):
        return pltpu.make_async_copy(weights.at[r], w.at[r], ld_w.at[r])

    def load_x(c, h):
        return pltpu.make_async_copy(
            acts.at[c, :, pl.ds(h * C, C)], xg.at[c, y * H + h], ld_x
        )

    load_c = pltpu.make_async_copy(cot, cotv, ld_c)

    @pl.when(first)
    def _():
        for h in range(H):
            lax.fori_loop(0, n, lambda c, u: (load_x(c, h).start(), u)[1], 0)

    lax.fori_loop(0, Z, lambda r, u: (load_w(r).start(), u)[1], 0)

    @pl.when(last)
    def _():
        load_c.start()

    ha = jnp.max(hist_act[...], axis=1, keepdims=True)
    hw = jnp.max(hist_weight[...], axis=1, keepdims=True)
    hg = jnp.max(hist_grad[...], axis=1, keepdims=True)
    act_factor = 448.0 / ha
    weight_factor = 448.0 / hw
    grad_factor = 57344.0 / hg
    forward_factor = 1.0 / (act_factor * weight_factor)
    backward_factor = 1.0 / (grad_factor * weight_factor)
    update_factor = 1.0 / (act_factor * grad_factor)

    amax[...] = jnp.zeros_like(amax)
    wmax[...] = jnp.zeros_like(wmax)
    gmax[...] = jnp.zeros_like(gmax)

    @pl.when(first)
    def _():
        pltpu.make_async_copy(xg.at[:, own], xg.at[:, own], ld_x).wait()


    def gather_copy(c, d):
        return rcopy(xg.at[c, own], xg.at[c, own], fg_send, f_recv.at[c, y], tensor=at_y(d))

    def out_copy(c, d):
        return rcopy(outv.at[c], xg.at[c, own], fo_send, f_recv.at[c, y], pipe=up, tensor=at_y(d))

    def wait_block(c, yb):
        drain_recv(f_recv.at[c, yb], xg.at[c, pl.ds(yb * H, H)])

    def act_copy(c, d):
        r = at_z(d)
        return rcopy(xq.at[c, r], ar.at[c, z], a_send, a_recv.at[(c == n - 1).astype(jnp.int32)], dp=r)

    def quant_w(r, u):
        load_w(r).wait()
        raw = w[r].astype(F32)
        wmax[...] = jnp.maximum(wmax[...], jnp.max(jnp.abs(raw), axis=0, keepdims=True))
        w[r] = jnp.clip(raw * weight_factor, -448.0, 448.0).astype(BF16)
        return u

    def turn_w(r, u):
        wt[r] = w[r].T
        return u

    with scope("qw"):
        lax.fori_loop(0, Z, quant_w, 0)

    with scope("barrier"):
        pairs = not_first.astype(jnp.int32) + not_last.astype(jnp.int32)
        pl.semaphore_wait(barrier, (T - 1) + (Z - 1) + T * pairs)

    def start_gather(c):
        for d in (2, 1, 3):
            gather_copy(c, d).start()

    @pl.when(first)
    def _():
        for c in range(AHEAD):
            start_gather(c)

    late = s >= S // 2
    early = jnp.logical_not(late)

    @pl.when(late)
    def _():
        with scope("turn"):
            lax.fori_loop(0, Z, turn_w, 0)

    def store_out(c, h):
        return pltpu.make_async_copy(outv.at[c, h], out_acts.at[c, :, pl.ds(h * C, C)], st_o)

    def forward(c):
        @pl.when(first & (c + AHEAD < n))
        def _():
            start_gather(c + AHEAD)

        total = jnp.zeros((R, H * C), F32)
        for j in range(T):
            yb = at_y((2 * (1 - odd), 1, 3, 2 * odd)[j])

            if j < T - 1:
                with scope(f"fwait{j}"):
                    wait_block(c, yb)
            else:
                @pl.when(not_first)
                def _():
                    with scope(f"fwait{j}"):
                        wait_block(c, yb)

            for h in range(H):
                r = yb * H + h
                x = xg[c, r]
                q = quantize(x, act_factor, 448.0)
                xq[c, r] = q
                total = total + jnp.dot(q, w[r], preferred_element_type=F32)
        for h in range(H):
            x = xg[c, y * H + h].astype(F32)
            outv[c, h] = (x + total[:, h * C : (h + 1) * C] * forward_factor).astype(BF16)

        @pl.when(not_last)
        def _():
            for d in (2, 1, 3, 0):
                out_copy(c, d).start()

        with scope("fz"):
            for d in (4, 3, 5, 2, 6, 1, 7):
                act_copy(c, d).start()
            ar[c, z] = xq[c, z]
            for h in range(H):
                store_out(c, h).start()
                x = xg[c, y * H + h].astype(F32)
                amax[h] = jnp.maximum(amax[h], jnp.max(jnp.abs(x), axis=0, keepdims=True))

    def part_copy(c, d):
        yb = at_y(d)
        return rcopy(ps.at[c, yb], pr.at[c, y], p_send, p_recv.at[c], pipe=down, tensor=yb)

    def peer_copy(c, d):
        yb = at_y(d)
        return rcopy(ps.at[c, yb], pr0.at[c, y], p_send, p0_recv, tensor=yb)

    def back_copy(c):
        return rcopy(gin.at[c], gout.at[c], go_send, go_recv, pipe=up)

    def z_copy(c, d):
        if d == 2:
            recv = zf_recv.at[c, 0]
        elif d == Z - 2:
            recv = zf_recv.at[c, 1]
        else:
            recv = zo_recv.at[(c == n - 1).astype(jnp.int32)]
        return rcopy(gq.at[c], gr.at[c, z], z_send, recv, dp=at_z(d))

    def relay_copies(c):
        lo, hi = at_z(Z - 2), at_z(2)
        half = H * C // 2
        out = []
        for k, dest, part in (
            (lo, 1, pl.ds(0, 2 * half)), (hi, Z - 1, pl.ds(0, 2 * half)),
            (lo, 2, pl.ds(0, half)), (hi, Z - 2, pl.ds(half, half)),
        ):
            ref = gr.at[c, k, :, part]
            out.append(rcopy(ref, ref, z_send, zo_recv.at[0], dp=at_z(dest)))
        return out

    def wait_far(c):
        drain_recv(zf_recv.at[c, 0], gr.at[c, at_z(Z - 2)])
        drain_recv(zf_recv.at[c, 1], gr.at[c, at_z(2)])

    def relay(c):
        with scope("relay"):
            wait_far(c)
            for r in relay_copies(c):
                r.start()

    def store_g(c):
        return pltpu.make_async_copy(gout.at[c], out_grads.at[c], st_g)

    @pl.when(last)
    def _():
        load_c.wait()

    def backward(c):
        @pl.when(last)
        def _():
            for h in range(H):
                part = cotv[c, :, h * C : (h + 1) * C].astype(F32) * outv[c, h].astype(F32)
                gin[c, :, h * C : (h + 1) * C] = part.astype(BF16)

        @pl.when(not_last)
        def _():
            with scope("bwait"):
                drain_recv(p_recv.at[c], pr.at[c])
            for h in range(H):
                g = pr[c, 0, h].astype(F32)
                for k in range(1, T):
                    g = g + pr[c, k, h].astype(F32)
                gin[c, :, h * C : (h + 1) * C] = g.astype(BF16)

        g = gin[c]
        q = quantize(g, grad_factor, 57344.0)
        gq[c] = q

        for d in (2, 1, 3, 0):
            yb = at_y(d)
            for h in range(H):
                part = jnp.dot(q, wt[yb * H + h], preferred_element_type=F32) * backward_factor
                if d == 0:
                    part = part + g[:, h * C : (h + 1) * C].astype(F32)
                ps[c, yb, h] = part.astype(BF16)

            @pl.when(not_first)
            def _():
                part_copy(c, d).start()

            if d:
                @pl.when(first)
                def _():
                    peer_copy(c, d).start()

        with scope("bz"):
            for d in (2, Z - 2, 1, Z - 1):
                z_copy(c, d).start()

            @pl.when(c == n - 1)
            def _():
                for d in range(3, Z - 2):
                    z_copy(c, d).start()

            @pl.when(not_last)
            def _():
                back_copy(c).start()

            gmax[...] = jnp.maximum(gmax[...], jnp.max(jnp.abs(g.astype(F32)), axis=0, keepdims=True))
            gr[c, z] = q

        @pl.when((c >= LAG) & early)
        def _():
            relay(c - LAG)

    def slot(k, u):
        ahead = jnp.where(last, lax.rem(k, 2) == 0, k < n)
        c = jnp.where(last, k // 2, lax.rem(k, n))

        @pl.when(ahead)
        def _():
            forward(c)

        @pl.when(jnp.logical_not(ahead))
        def _():
            backward(c)

        @pl.when(early & (k == n - 1))
        def _():
            with scope("turn"):
                lax.fori_loop(0, Z, turn_w, 0)

        return u

    lax.fori_loop(0, 2 * n, slot, 0)
    lax.fori_loop(jnp.where(early, n - LAG, 0), n - 1, lambda c, u: (relay(c), u)[1], 0)

    lanes = pks.shape[-1]
    peak_a = jnp.max(jnp.maximum(amax[0], amax[H - 1]), axis=1, keepdims=True)
    peak_w = jnp.max(wmax[...], axis=1, keepdims=True)
    peak_g = jnp.max(gmax[...], axis=1, keepdims=True)
    row = lax.broadcasted_iota(jnp.int32, (8, lanes), 0)
    tile = jnp.where(row == 0, peak_a, jnp.where(row == 1, peak_w, peak_g))
    pks[...] = tile

    def ky_copy(d):
        return rcopy(pks, pky.at[y], ky_send, ky_recv, tensor=at_y(d))

    def kz_copy(d):
        return rcopy(pkm, pkz.at[z], kz_send, kz_recv, dp=at_z(d))

    for d in range(1, T):
        ky_copy(d).start()
    with scope("kwait"):
        drain_recv(ky_recv, pky.at[pl.ds(0, T - 1)])
    pky[y] = tile
    for k in range(T):
        tile = jnp.maximum(tile, pky[k])
    pkm[...] = tile
    for d in range(1, Z):
        kz_copy(d).start()

    @pl.when(first)
    def _():
        def finish(c, u):
            for h in range(H):
                g = ps[c, y, h].astype(F32)
                for d in range(1, T):
                    g = g + pr0[c, at_y(d), h].astype(F32)
                gout[c, :, h * C : (h + 1) * C] = g.astype(BF16)
            return u

        with scope("first"):
            drain_recv(p0_recv, pr0.at[:, pl.ds(0, T - 1)])
            lax.fori_loop(0, n, finish, 0)

    @pl.when(not_first)
    def _():
        with scope("backwait"):
            drain_recv(go_recv, gout)

    lax.fori_loop(0, n, lambda c, u: (store_g(c).start(), u)[1], 0)

    def rows_product(lo, count):
        left = ar[lo : lo + count].reshape(count * Z * R, C)
        right = gr[lo : lo + count].reshape(count * Z * R, H * C)
        return lax.dot_general(left, right, (((0,), (0,)), ((), ())), preferred_element_type=F32)

    with scope("zwait"):
        drain_recv(a_recv.at[0], ar.at[pl.ds(0, n - 1), pl.ds(0, Z - 1)])
        drain_recv(zo_recv.at[0], gr.at[pl.ds(0, n - 1), pl.ds(0, Z - 3)])
    with scope("wgrad"):
        acc[...] = rows_product(0, n - 1)
    with scope("zwait_last"):
        drain_recv(a_recv.at[1], ar.at[n - 1, pl.ds(0, Z - 1)])
        drain_recv(zo_recv.at[1], gr.at[n - 1, pl.ds(0, Z - 3)])
        wait_far(n - 1)
    with scope("wgrad_last"):
        wg[...] = ((acc[...] + rows_product(n - 1, 1)) * update_factor).astype(BF16)
    st = pltpu.make_async_copy(wg, out_wgrad, st_w)
    st.start()

    drain_recv(kz_recv, pkz.at[pl.ds(0, Z - 1)])
    pkz[z] = tile
    for k in range(Z):
        tile = jnp.maximum(tile, pkz[k])
    out_peaks[...] = tile

    with scope("close"):
        drain_send(ky_send, pky.at[pl.ds(0, T - 1)])
        drain_send(kz_send, pkz.at[pl.ds(0, Z - 1)])
        drain_send(a_send, ar.at[:, pl.ds(0, Z - 1)])
        drain_send(z_send, gr.at[:, pl.ds(0, Z - 1)])

        @pl.when(first)
        def _():
            drain_send(fg_send, pr.at[:, pl.ds(0, T - 1)])
            drain_send(p_send, pr.at[:, pl.ds(0, T - 1)])

        @pl.when(not_first)
        def _():
            drain_send(p_send, pr)

        @pl.when(not_last)
        def _():
            drain_send(fo_send, pr)
            drain_send(go_send, gin)

        pltpu.make_async_copy(outv, outv, st_o).wait()
        pltpu.make_async_copy(gout, gout, st_g).wait()
        st.wait()


def finish_kernel(a, g, m, peaks, ha, hw, hg, oa, og, om, na, nw, ng, va, vg, vm, load, store):
    loads = [pltpu.make_async_copy(x, v, load.at[i]) for i, (x, v) in enumerate(((a, va), (g, vg), (m, vm)))]
    stores = [pltpu.make_async_copy(v, o, store.at[i]) for i, (v, o) in enumerate(((va, oa), (vg, og), (vm, om)))]
    for c in loads:
        c.start()
    for i, (old, new) in enumerate(((ha, na), (hw, nw), (hg, ng))):
        new[:, 1:] = old[:, :-1]
        new[:, 0:1] = peaks[i : i + 1, 0:1]
    for c, d in zip(loads, stores):
        c.wait()
        d.start()
    for d in stores:
        d.wait()


def step(acts_in, weights, cotangent, hist_act, hist_weight, hist_grad):
    S, Z, T = (lax.axis_size(a) for a in ("pipe", "dp", "tensor"))
    micro, rows, width = acts_in.shape
    depth = weights.shape[1]
    R = min(CHUNK, rows)
    n = micro * rows // R
    H = Z // T
    C = depth // Z
    acts = acts_in.reshape(n, R, width)
    cot = cotangent.reshape(n, R, width)
    w = weights.reshape(Z, C, width)
    any_ = pl.BlockSpec(memory_space=pl.ANY)
    hbm = pl.BlockSpec(memory_space=pltpu.HBM)
    vmem = pl.BlockSpec(memory_space=pltpu.VMEM)
    dma = pltpu.SemaphoreType.DMA
    b = lambda *shape: pltpu.VMEM(shape, BF16)
    f = lambda *shape: pltpu.VMEM(shape, F32)
    out_acts, out_grads, out_w, peaks = pl.pallas_call(
        functools.partial(kernel, S, Z, T, n, R),
        out_shape=(
            jax.ShapeDtypeStruct((n, R, width), BF16),
            jax.ShapeDtypeStruct((n, R, width), BF16),
            jax.ShapeDtypeStruct((C, width), BF16),
            jax.ShapeDtypeStruct((8, 128), F32),
        ),
        in_specs=[any_, any_, any_, vmem, vmem, vmem],
        out_specs=(any_, any_, any_, vmem),
        scratch_shapes=[
            b(Z, C, width), b(Z, width, C), b(n, Z, R, C), b(n, Z, R, C), b(n, Z, R, C), b(n, Z, R, width),
            b(n, H, R, C), b(n, R, width), b(n, R, width), b(n, R, width),
            b(n, T, H, R, C), b(n, T, H, R, C), b(n, T, H, R, C), b(n, R, width), f(C, width),
            b(C, width), f(H, 1, C), f(1, width), f(1, width),
            f(8, 128), f(T, 8, 128), f(8, 128), f(Z, 8, 128),
            dma((Z,)), *(dma,) * 5,
            dma((n, T)), dma, dma, dma, dma((2,)), dma, dma((n,)), dma, dma, dma, dma, dma((n, 2)), dma((2,)),
            *(dma,) * 4,
        ],
        compiler_params=pltpu.CompilerParams(
            collective_id=0, has_side_effects=True, vmem_limit_bytes=60 * 1024 * 1024
        ),
    )(acts, w, cot, hist_act, hist_weight, hist_grad)

    final = pl.pallas_call(
        finish_kernel,
        out_shape=(
            jax.ShapeDtypeStruct((n, R, width), BF16),
            jax.ShapeDtypeStruct((n, R, width), BF16),
            jax.ShapeDtypeStruct((C, width), BF16),
            *(jax.ShapeDtypeStruct(hist_act.shape, F32) for _ in range(3)),
        ),
        in_specs=[hbm, hbm, hbm, vmem, vmem, vmem, vmem],
        out_specs=(hbm, hbm, hbm, vmem, vmem, vmem),
        scratch_shapes=[b(n, R, width), b(n, R, width), b(C, width), dma((3,)), dma((3,))],
        compiler_params=pltpu.CompilerParams(vmem_limit_bytes=8 * 1024 * 1024),
    )(out_acts, out_grads, out_w, peaks, hist_act, hist_weight, hist_grad)
    return (
        final[0].reshape(1, micro, rows, width),
        final[1].reshape(1, micro, rows, width),
        final[2][None],
        *final[3:],
    )


def solution(mesh):
    placed = (
        P(None, "dp", "tensor"),
        P("pipe", None, "tensor"),
        P(None, "dp", "tensor"),
        P("pipe", None),
        P("pipe", None),
        P("pipe", None),
    )
    return jax.shard_map(
        step,
        mesh=mesh,
        in_specs=placed,
        out_specs=(
            P("pipe", None, "dp", "tensor"),
            P("pipe", None, "dp", "tensor"),
            P("pipe", "dp", "tensor"),
            P("pipe", None),
            P("pipe", None),
            P("pipe", None),
        ),
        check_vma=False,
    )
```

time: 276 us -> 165 us (0.60)
  Pallas kernels: 262 us -> 160 us
  local copies, waits for them, and re-layouts: 7.33 us -> 3.99 us
  other arithmetic: 3.11 us -> 0 us
    pallas_call x1, Pallas kernels: 262 us -> 158 us  [step(): pl.pallas_call(functools.partial(kernel, S, Z, T, n, R), out_shape=(jax.S...]
    concatenate x2 -> x0, other arithmetic: 3.11 us -> none  [roll(): return jnp.concatenate([newest, history[:, :-1]], axis=1)]
    unnamed x9 -> x14, local copies, waits for them, and re-layouts: 6.01 us -> 3.99 us
where the time goes in v2:
time: 165 us
  Pallas kernels  160 us (97%)
  local copies, waits for them, and re-layouts  3.99 us (2%)
    pallas_call x1, Pallas kernels, step(): pl.pallas_call(functools.partial(kernel, S, Z, T, n, R), out_shape=(jax.S...  158 us
    unnamed x14, local copies, waits for them, and re-layouts  3.99 us

profile of v2, /device:TPU:32, one launch (start us, length us, event | category | flops | bytes accessed | tf_op | source)
XLA Modules:
  0.0 165.1 jit_solution(15920934433867743659)
XLA Ops:
  0.6 0.0 copy-start.6
  0.6 0.0 copy-start.5
  0.7 0.0 copy-start.4
  0.7 158.3 %shard_map.109 = (bf16[16,16,1024]{2,1,0:T(8,128)(2,1)}, bf16[16,16,1024]{2,1,0:T(8,128)(2,1)}, bf16[512,1024]{1,0:T(8,128)(2,1)}, f32[8,128]{1,0:T(8,128)}) custom-call(bf16[16,16,1024]{2,1,0:T(8,128)(2,1)} %bitcast.7, bf16[8,512,1024]{2,1,0:T(8,128)(2,1)} %bitcast.6, bf16[16,16,1024]{2,1,0:T(8,128)(2,1)} %bitcast.8, f32[1,16]{1,0:T(1,128)} %ha.1, ...), custom_call_target="tpu_custom_call" | custom-call | tf_op jit(solution)/shard_map/pallas_call | solution.py:476
  159.0 0.0 copy-done.6
  159.0 0.0 copy-done.5
  159.0 0.0 copy-done.4
  159.1 0.0 copy-start
  159.1 1.2 copy-done
  160.3 0.0 copy-start.1
  160.3 1.0 copy-done.1
  161.3 0.0 copy-start.2
  161.3 1.0 copy-done.2
  162.4 0.0 copy-start.3
  162.4 0.7 copy-done.3
  163.0 2.1 %shard_map.110 = (bf16[16,16,1024]{2,1,0:T(8,128)(2,1)}, bf16[16,16,1024]{2,1,0:T(8,128)(2,1)}, bf16[512,1024]{1,0:T(8,128)(2,1)}, f32[1,16]{1,0:T(1,128)}, f32[1,16]{1,0:T(1,128)}, /*index=5*/f32[1,16]{1,0:T(1,128)}) custom-call(bf16[16,16,1024]{2,1,0:T(8,128)(2,1)S(1)} %copy-done.1, bf16[16,16,1024]{2,1,0:T(8,128)(2,1)S(1)} %copy-done.2, ...), custom_call_target="tpu_custom_call" | custom-call | tf_op jit(solution)/shard_map/pallas_call | solution.py:501
Async XLA Ops:
  0.6 158.4 %copy-start.6 = (f32[1,16]{1,0:T(1,128)S(1)}, f32[1,16]{1,0:T(1,128)}, u32[]{:S(2)}) copy-start(f32[1,16]{1,0:T(1,128)} %hg.1) | copy-start | bytes 196
  0.6 158.4 %copy-start.5 = (f32[1,16]{1,0:T(1,128)S(1)}, f32[1,16]{1,0:T(1,128)}, u32[]{:S(2)}) copy-start(f32[1,16]{1,0:T(1,128)} %hw.1) | copy-start | bytes 196
  0.7 158.4 %copy-start.4 = (f32[1,16]{1,0:T(1,128)S(1)}, f32[1,16]{1,0:T(1,128)}, u32[]{:S(2)}) copy-start(f32[1,16]{1,0:T(1,128)} %ha.1) | copy-start | bytes 196
  159.1 1.2 copy-start
  160.3 1.0 copy-start.1
  161.3 1.0 copy-start.2
  162.4 0.7 copy-start.3

commit v3 on v2

--- a/solution.py
+++ b/solution.py
@@ -12,8 +12,8 @@
 F32 = jnp.float32
 BF16 = jnp.bfloat16
 CHUNK = 16
-AHEAD = 3
-LAG = 4
+AHEAD = 5
+WARM = 8
 
 scope = lambda name: contextlib.nullcontext()
 
@@ -30,9 +30,10 @@
     S, Z, T, n, R,
     acts, weights, cot, hist_act, hist_weight, hist_grad,
     out_acts, out_grads, out_wgrad, out_peaks,
-    w, wt, xg, xq, ar, gr, outv, gin, gout, gq, ps, pr, pr0, cotv, acc, wg, amax, wmax, gmax, pks, pky, pkm, pkz,
+    w, wt, xg, xq, ar, gr, outv, gin, gout, gq, ps, pr, cotv, acc, wg, amax, wmax, gmax, pks, pky, pkm, pkz,
     ld_w, ld_x, ld_c, st_o, st_g, st_w,
-    f_recv, fg_send, fo_send, a_send, a_recv, p_send, p_recv, p0_recv, go_send, go_recv, z_send, zf_recv, zo_recv,
+    f_recv, fg_send, fo_send, a_send, a_recv, ay_send, ay_recv, p_send, p_recv, go_send, go_recv,
+    z_send, zr_recv, zo_recv,
     ky_send, ky_recv, kz_send, kz_recv,
 ):
     s = lax.axis_index("pipe")
@@ -40,6 +41,8 @@
     y = lax.axis_index("tensor")
     H = Z // T
     C = w.shape[1]
+    U = n // 2
+    Q = n // T
     odd = lax.rem(s, 2)
     even = odd == 0
     is_odd = odd == 1
@@ -132,9 +135,20 @@
     def wait_block(c, yb):
         drain_recv(f_recv.at[c, yb], xg.at[c, pl.ds(yb * H, H)])
 
-    def act_copy(c, d):
+    def act_copy(c, m, d):
         r = at_z(d)
-        return rcopy(xq.at[c, r], ar.at[c, z], a_send, a_recv.at[(c == n - 1).astype(jnp.int32)], dp=r)
+        span = pl.ds(c, m)
+        return rcopy(xq.at[span, r], ar.at[span, z], a_send, a_recv, dp=r)
+
+    def share_copy(d):
+        span = pl.ds(y * Q, Q)
+        return rcopy(ar.at[span], ar.at[span], ay_send, ay_recv, tensor=at_y(d))
+
+    def share_acts():
+        with scope("share"):
+            drain_recv(a_recv, ar.at[pl.ds(0, Q), pl.ds(0, Z - 1)])
+            for d in (2, 1, 3):
+                share_copy(d).start()
 
     def quant_w(r, u):
         load_w(r).wait()
@@ -143,8 +157,9 @@
         w[r] = jnp.clip(raw * weight_factor, -448.0, 448.0).astype(BF16)
         return u
 
-    def turn_w(r, u):
-        wt[r] = w[r].T
+    def turn_w(k, u):
+        for h in range(H):
+            wt[k, :, h * C : (h + 1) * C] = w[k * H + h].T
         return u
 
     with scope("qw"):
@@ -169,94 +184,104 @@
     @pl.when(late)
     def _():
         with scope("turn"):
-            lax.fori_loop(0, Z, turn_w, 0)
+            lax.fori_loop(0, T, turn_w, 0)
 
     def store_out(c, h):
         return pltpu.make_async_copy(outv.at[c, h], out_acts.at[c, :, pl.ds(h * C, C)], st_o)
 
-    def forward(c):
-        @pl.when(first & (c + AHEAD < n))
-        def _():
-            start_gather(c + AHEAD)
-
-        total = jnp.zeros((R, H * C), F32)
+    def forward(c, m):
+        span = pl.ds(c, m)
+        total = jnp.zeros((m * R, H * C), F32)
         for j in range(T):
             yb = at_y((2 * (1 - odd), 1, 3, 2 * odd)[j])
 
-            if j < T - 1:
+            def take():
                 with scope(f"fwait{j}"):
-                    wait_block(c, yb)
+                    for i in range(m):
+                        wait_block(c + i, yb)
+
+            if m > 1 or j < T - 1:
+                take()
             else:
-                @pl.when(not_first)
-                def _():
-                    with scope(f"fwait{j}"):
-                        wait_block(c, yb)
+                pl.when(not_first)(take)
 
             for h in range(H):
                 r = yb * H + h
-                x = xg[c, r]
-                q = quantize(x, act_factor, 448.0)
-                xq[c, r] = q
+                q = quantize(xg[span, r].reshape(m * R, C), act_factor, 448.0)
+                xq[span, r] = q.reshape(m, R, C)
                 total = total + jnp.dot(q, w[r], preferred_element_type=F32)
         for h in range(H):
-            x = xg[c, y * H + h].astype(F32)
-            outv[c, h] = (x + total[:, h * C : (h + 1) * C] * forward_factor).astype(BF16)
-
-        @pl.when(not_last)
-        def _():
-            for d in (2, 1, 3, 0):
-                out_copy(c, d).start()
+            x = xg[span, y * H + h].reshape(m * R, C).astype(F32)
+            o = x + total[:, h * C : (h + 1) * C] * forward_factor
+            outv[span, h] = o.astype(BF16).reshape(m, R, C)
+
+        def send():
+            for i in range(m):
+                for d in (2, 1, 3, 0):
+                    out_copy(c + i, d).start()
+
+        if m == 1:
+            send()
+        else:
+            pl.when(not_last)(send)
 
         with scope("fz"):
-            for d in (4, 3, 5, 2, 6, 1, 7):
-                act_copy(c, d).start()
-            ar[c, z] = xq[c, z]
+            if m == 1:
+                @pl.when(first & (c + AHEAD < n))
+                def _():
+                    start_gather(c + AHEAD)
+
+            @pl.when(c // Q == y)
+            def _():
+                for d in (4, 3, 5, 2, 6, 1, 7):
+                    act_copy(c, m, d).start()
+                ar[span, z] = xq[span, z]
+
             for h in range(H):
-                store_out(c, h).start()
-                x = xg[c, y * H + h].astype(F32)
+                for i in range(m):
+                    store_out(c + i, h).start()
+                x = xg[span, y * H + h].reshape(m * R, C).astype(F32)
                 amax[h] = jnp.maximum(amax[h], jnp.max(jnp.abs(x), axis=0, keepdims=True))
+
+    side = first.astype(jnp.int32)
 
     def part_copy(c, d):
         yb = at_y(d)
-        return rcopy(ps.at[c, yb], pr.at[c, y], p_send, p_recv.at[c], pipe=down, tensor=yb)
-
-    def peer_copy(c, d):
-        yb = at_y(d)
-        return rcopy(ps.at[c, yb], pr0.at[c, y], p_send, p0_recv, tensor=yb)
+        recv = p_recv.at[jnp.where(first, n, c)]
+        return rcopy(ps.at[c, yb], pr.at[side, c, y], p_send, recv, pipe=down, tensor=yb)
 
     def back_copy(c):
         return rcopy(gin.at[c], gout.at[c], go_send, go_recv, pipe=up)
 
-    def z_copy(c, d):
-        if d == 2:
-            recv = zf_recv.at[c, 0]
-        elif d == Z - 2:
-            recv = zf_recv.at[c, 1]
+    def ring_copy(u, back):
+        span = pl.ds(2 * u, 2)
+        return rcopy(gq.at[span], gr.at[span, z], z_send, zr_recv.at[u, 3 * back], dp=at_z(Z - 1 if back else 1))
+
+    def relay_copy(u, level, back):
+        k = at_z(level if back else Z - level)
+        span = pl.ds(2 * u, 2)
+        if level < 3:
+            ref = gr.at[span, k]
+            recv = zr_recv.at[u, 3 * back + level]
         else:
-            recv = zo_recv.at[(c == n - 1).astype(jnp.int32)]
-        return rcopy(gq.at[c], gr.at[c, z], z_send, recv, dp=at_z(d))
-
-    def relay_copies(c):
-        lo, hi = at_z(Z - 2), at_z(2)
-        half = H * C // 2
-        out = []
-        for k, dest, part in (
-            (lo, 1, pl.ds(0, 2 * half)), (hi, Z - 1, pl.ds(0, 2 * half)),
-            (lo, 2, pl.ds(0, half)), (hi, Z - 2, pl.ds(half, half)),
-        ):
-            ref = gr.at[c, k, :, part]
-            out.append(rcopy(ref, ref, z_send, zo_recv.at[0], dp=at_z(dest)))
-        return out
-
-    def wait_far(c):
-        drain_recv(zf_recv.at[c, 0], gr.at[c, at_z(Z - 2)])
-        drain_recv(zf_recv.at[c, 1], gr.at[c, at_z(2)])
-
-    def relay(c):
-        with scope("relay"):
-            wait_far(c)
-            for r in relay_copies(c):
-                r.start()
+            half = H * C // 2
+            ref = gr.at[span, k, :, pl.ds(half * back, half)]
+            recv = zo_recv.at[u]
+        return rcopy(ref, ref, z_send, recv, dp=at_z(Z - 1 if back else 1))
+
+    lag = jnp.where(s < 2, 1, 2)
+
+    def relays(t):
+        for level in (1, 2, 3):
+            u = t - lag * level
+
+            @pl.when((u >= 0) & (u < U))
+            def _():
+                with scope(f"relay{level}"):
+                    for back in (0, 1):
+                        k = at_z(level if back else Z - level)
+                        drain_recv(zr_recv.at[u, 3 * back + level - 1], gr.at[pl.ds(2 * u, 2), k])
+                        relay_copy(u, level, back).start()
 
     def store_g(c):
         return pltpu.make_async_copy(gout.at[c], out_grads.at[c], st_g)
@@ -265,85 +290,109 @@
     def _():
         load_c.wait()
 
-    def backward(c):
-        @pl.when(last)
-        def _():
+    def backward(c, m):
+        span = pl.ds(c, m)
+        def begin():
             for h in range(H):
-                part = cotv[c, :, h * C : (h + 1) * C].astype(F32) * outv[c, h].astype(F32)
-                gin[c, :, h * C : (h + 1) * C] = part.astype(BF16)
-
-        @pl.when(not_last)
-        def _():
+                part = cotv[span, :, h * C : (h + 1) * C].astype(F32) * outv[span, h].astype(F32)
+                gin[span, :, h * C : (h + 1) * C] = part.astype(BF16)
+
+        def arrive():
             with scope("bwait"):
-                drain_recv(p_recv.at[c], pr.at[c])
+                for i in range(m):
+                    drain_recv(p_recv.at[c + i], pr.at[0, c + i])
             for h in range(H):
-                g = pr[c, 0, h].astype(F32)
+                g = pr[0, span, 0, h].astype(F32)
                 for k in range(1, T):
-                    g = g + pr[c, k, h].astype(F32)
-                gin[c, :, h * C : (h + 1) * C] = g.astype(BF16)
-
-        g = gin[c]
+                    g = g + pr[0, span, k, h].astype(F32)
+                gin[span, :, h * C : (h + 1) * C] = g.astype(BF16)
+
+        if m > 1:
+            pl.when(last)(begin)
+            pl.when(not_last)(arrive)
+        else:
+            arrive()
+        g = gin[span].reshape(m * R, H * C)
         q = quantize(g, grad_factor, 57344.0)
-        gq[c] = q
-
+        gq[span] = q.reshape(m, R, H * C)
         for d in (2, 1, 3, 0):
             yb = at_y(d)
+            part = jnp.dot(q, wt[yb], preferred_element_type=F32) * backward_factor
+            if d == 0:
+                part = part + g.astype(F32)
             for h in range(H):
-                part = jnp.dot(q, wt[yb * H + h], preferred_element_type=F32) * backward_factor
-                if d == 0:
-                    part = part + g[:, h * C : (h + 1) * C].astype(F32)
-                ps[c, yb, h] = part.astype(BF16)
-
-            @pl.when(not_first)
-            def _():
-                part_copy(c, d).start()
-
+                ps[span, yb, h] = part[:, h * C : (h + 1) * C].astype(BF16).reshape(m, R, C)
             if d:
-                @pl.when(first)
-                def _():
-                    peer_copy(c, d).start()
-
-        with scope("bz"):
-            for d in (2, Z - 2, 1, Z - 1):
-                z_copy(c, d).start()
-
-            @pl.when(c == n - 1)
-            def _():
-                for d in range(3, Z - 2):
-                    z_copy(c, d).start()
+                for i in range(m):
+                    part_copy(c + i, d).start()
+
+        def to_own():
+            for i in range(m):
+                part_copy(c + i, 0).start()
+
+        if m > 1:
+            to_own()
 
             @pl.when(not_last)
             def _():
-                back_copy(c).start()
-
+                for i in range(m):
+                    back_copy(c + i).start()
+        else:
+            pl.when(not_first)(to_own)
+            back_copy(c).start()
+        with scope("bz"):
             gmax[...] = jnp.maximum(gmax[...], jnp.max(jnp.abs(g.astype(F32)), axis=0, keepdims=True))
-            gr[c, z] = q
-
-        @pl.when((c >= LAG) & early)
-        def _():
-            relay(c - LAG)
+            gr[span, z] = q.reshape(m, R, H * C)
+
+    prior = s == S - 2
+    inner = not_last & jnp.logical_not(prior)
+    warm = jnp.where(last, 0, jnp.where(prior, WARM, n))
 
     def slot(k, u):
-        ahead = jnp.where(last, lax.rem(k, 2) == 0, k < n)
-        c = jnp.where(last, k // 2, lax.rem(k, n))
+        ahead = k < warm
+        pairs = jnp.logical_not(ahead) & jnp.logical_not(inner)
+        late_k = k - warm
+        mixed = jnp.logical_not(ahead) & (late_k < n - warm)
+        turn = lax.rem(late_k, 2)
+        fwd_pair = pairs & mixed & jnp.where(last, turn == 0, turn == 1)
+        bwd_pair = pairs & jnp.logical_not(fwd_pair)
+        bwd_one = jnp.logical_not(ahead) & inner
+        f_at = warm + 2 * (late_k // 2)
+        b_at = jnp.where(mixed, 2 * (late_k // 2), n - warm + 2 * (late_k - (n - warm)))
 
         @pl.when(ahead)
         def _():
-            forward(c)
-
-        @pl.when(jnp.logical_not(ahead))
-        def _():
-            backward(c)
+            forward(k, 1)
+
+        @pl.when(fwd_pair)
+        def _():
+            forward(f_at, 2)
+
+        @pl.when(bwd_pair)
+        def _():
+            backward(b_at, 2)
+
+        @pl.when(bwd_one)
+        def _():
+            backward(late_k, 1)
+
+        unit = jnp.where(inner, late_k, b_at) // 2
+
+        @pl.when(bwd_pair | (bwd_one & (lax.rem(late_k, 2) == 1)))
+        def _():
+            ring_copy(unit, 0).start()
+            ring_copy(unit, 1).start()
+            relays(unit)
 
         @pl.when(early & (k == n - 1))
         def _():
             with scope("turn"):
-                lax.fori_loop(0, Z, turn_w, 0)
+                lax.fori_loop(0, T, turn_w, 0)
+            share_acts()
 
         return u
 
-    lax.fori_loop(0, 2 * n, slot, 0)
-    lax.fori_loop(jnp.where(early, n - LAG, 0), n - 1, lambda c, u: (relay(c), u)[1], 0)
+    lax.fori_loop(0, jnp.where(inner, 2 * n, jnp.where(last, n, n + WARM // 2)), slot, 0)
 
     lanes = pks.shape[-1]
     peak_a = jnp.max(jnp.maximum(amax[0], amax[H - 1]), axis=1, keepdims=True)
@@ -361,6 +410,37 @@
 
     for d in range(1, T):
         ky_copy(d).start()
+
+    def rows_product(lo, count):
+        left = ar[lo : lo + count].reshape(count * Z * R, C)
+        right = gr[lo : lo + count].reshape(count * Z * R, H * C)
+        return lax.dot_general(left, right, (((0,), (0,)), ((), ())), preferred_element_type=F32)
+
+    def wait_opposite(lo, hi):
+        for u in range(lo, hi):
+            drain_recv(zo_recv.at[u], gr.at[pl.ds(2 * u, 2), 0])
+
+    def first_rows():
+        with scope("wgrad"):
+            drain_recv(ay_recv, ar.at[pl.ds(0, (T - 1) * Q)])
+            wait_opposite(0, U // 2)
+            acc[...] = rows_product(0, n // 2)
+
+    def rest(k, u):
+        relays(k)
+
+        @pl.when(late & (k == U + 1))
+        def _():
+            share_acts()
+
+        @pl.when(early & (k == U - 1 + lag))
+        def _():
+            first_rows()
+
+        return u
+
+    lax.fori_loop(U, U + 3 * lag, rest, 0)
+
     with scope("kwait"):
         drain_recv(ky_recv, pky.at[pl.ds(0, T - 1)])
     pky[y] = tile
@@ -376,12 +456,12 @@
             for h in range(H):
                 g = ps[c, y, h].astype(F32)
                 for d in range(1, T):
-                    g = g + pr0[c, at_y(d), h].astype(F32)
+                    g = g + pr[1, c, at_y(d), h].astype(F32)
                 gout[c, :, h * C : (h + 1) * C] = g.astype(BF16)
             return u
 
         with scope("first"):
-            drain_recv(p0_recv, pr0.at[:, pl.ds(0, T - 1)])
+            drain_recv(p_recv.at[n], pr.at[1, :, pl.ds(0, T - 1)])
             lax.fori_loop(0, n, finish, 0)
 
     @pl.when(not_first)
@@ -391,22 +471,14 @@
 
     lax.fori_loop(0, n, lambda c, u: (store_g(c).start(), u)[1], 0)
 
-    def rows_product(lo, count):
-        left = ar[lo : lo + count].reshape(count * Z * R, C)
-        right = gr[lo : lo + count].reshape(count * Z * R, H * C)
-        return lax.dot_general(left, right, (((0,), (0,)), ((), ())), preferred_element_type=F32)
-
-    with scope("zwait"):
-        drain_recv(a_recv.at[0], ar.at[pl.ds(0, n - 1), pl.ds(0, Z - 1)])
-        drain_recv(zo_recv.at[0], gr.at[pl.ds(0, n - 1), pl.ds(0, Z - 3)])
-    with scope("wgrad"):
-        acc[...] = rows_product(0, n - 1)
+    pl.when(late)(first_rows)
+    with scope("wgrad2"):
+        wait_opposite(U // 2, U - 1)
+        acc[...] += rows_product(n // 2, n // 2 - 2)
     with scope("zwait_last"):
-        drain_recv(a_recv.at[1], ar.at[n - 1, pl.ds(0, Z - 1)])
-        drain_recv(zo_recv.at[1], gr.at[n - 1, pl.ds(0, Z - 3)])
-        wait_far(n - 1)
+        wait_opposite(U - 1, U)
     with scope("wgrad_last"):
-        wg[...] = ((acc[...] + rows_product(n - 1, 1)) * update_factor).astype(BF16)
+        wg[...] = ((acc[...] + rows_product(n - 2, 2)) * update_factor).astype(BF16)
     st = pltpu.make_async_copy(wg, out_wgrad, st_w)
     st.start()
 
@@ -419,21 +491,22 @@
     with scope("close"):
         drain_send(ky_send, pky.at[pl.ds(0, T - 1)])
         drain_send(kz_send, pkz.at[pl.ds(0, Z - 1)])
-        drain_send(a_send, ar.at[:, pl.ds(0, Z - 1)])
+        drain_send(a_send, ar.at[pl.ds(0, Q), pl.ds(0, Z - 1)])
+        drain_send(ay_send, ar.at[pl.ds(0, (T - 1) * Q)])
         drain_send(z_send, gr.at[:, pl.ds(0, Z - 1)])
 
         @pl.when(first)
         def _():
-            drain_send(fg_send, pr.at[:, pl.ds(0, T - 1)])
-            drain_send(p_send, pr.at[:, pl.ds(0, T - 1)])
+            drain_send(fg_send, pr.at[0, :, pl.ds(0, T - 1)])
+            drain_send(p_send, pr.at[0, :, pl.ds(0, T - 1)])
 
         @pl.when(not_first)
         def _():
-            drain_send(p_send, pr)
+            drain_send(p_send, pr.at[0])
 
         @pl.when(not_last)
         def _():
-            drain_send(fo_send, pr)
+            drain_send(fo_send, pr.at[0])
             drain_send(go_send, gin)
 
         pltpu.make_async_copy(outv, outv, st_o).wait()
@@ -484,13 +557,13 @@
         in_specs=[any_, any_, any_, vmem, vmem, vmem],
         out_specs=(any_, any_, any_, vmem),
         scratch_shapes=[
-            b(Z, C, width), b(Z, width, C), b(n, Z, R, C), b(n, Z, R, C), b(n, Z, R, C), b(n, Z, R, width),
+            b(Z, C, width), b(T, width, width), b(n, Z, R, C), b(n, Z, R, C), b(n, Z, R, C), b(n, Z, R, width),
             b(n, H, R, C), b(n, R, width), b(n, R, width), b(n, R, width),
-            b(n, T, H, R, C), b(n, T, H, R, C), b(n, T, H, R, C), b(n, R, width), f(C, width),
+            b(n, T, H, R, C), b(2, n, T, H, R, C), b(n, R, width), f(C, width),
             b(C, width), f(H, 1, C), f(1, width), f(1, width),
             f(8, 128), f(T, 8, 128), f(8, 128), f(Z, 8, 128),
             dma((Z,)), *(dma,) * 5,
-            dma((n, T)), dma, dma, dma, dma((2,)), dma, dma((n,)), dma, dma, dma, dma, dma((n, 2)), dma((2,)),
+            dma((n, T)), *(dma,) * 7, dma((n + 1,)), dma, dma, dma, dma((n // 2, 6)), dma((n // 2,)),
             *(dma,) * 4,
         ],
         compiler_params=pltpu.CompilerParams(
@@ -509,7 +582,7 @@
         in_specs=[hbm, hbm, hbm, vmem, vmem, vmem, vmem],
         out_specs=(hbm, hbm, hbm, vmem, vmem, vmem),
         scratch_shapes=[b(n, R, width), b(n, R, width), b(C, width), dma((3,)), dma((3,))],
-        compiler_params=pltpu.CompilerParams(vmem_limit_bytes=8 * 1024 * 1024),
+        compiler_params=pltpu.CompilerParams(vmem_limit_bytes=60 * 1024 * 1024),
     )(out_acts, out_grads, out_w, peaks, hist_act, hist_weight, hist_grad)
     return (
         final[0].reshape(1, micro, rows, width),

time: 165 us -> 151 us (0.915)
  Pallas kernels: 160 us -> 150 us
  local copies, waits for them, and re-layouts: 3.99 us -> 0 us
    pallas_call x1, Pallas kernels: 158 us -> 146 us  [step(): pl.pallas_call(functools.partial(kernel, S, Z, T, n, R), out_shape=(jax.S...]
    unnamed x14 -> x0, local copies, waits for them, and re-layouts: 3.99 us -> none
    pallas_call x1, Pallas kernels: 2.1 us -> 3.79 us  [step(): pl.pallas_call(finish_kernel, out_shape=(jax.ShapeDtypeStruct((n, R, widt...]
where the time goes in v3:
time: 151 us
  Pallas kernels  150 us (99%)
    pallas_call x1, Pallas kernels, step(): pl.pallas_call(functools.partial(kernel, S, Z, T, n, R), out_shape=(jax.S...  146 us
    pallas_call x1, Pallas kernels, step(): pl.pallas_call(finish_kernel, out_shape=(jax.ShapeDtypeStruct((n, R, widt...  3.79 us

profile of v3, /device:TPU:32, one launch (start us, length us, event | category | flops | bytes accessed | tf_op | source)
XLA Modules:
  0.0 150.5 jit_solution(8268465478666062747)
XLA Ops:
  0.6 146.1 %shard_map.109 = (bf16[16,16,1024]{2,1,0:T(8,128)(2,1)}, bf16[16,16,1024]{2,1,0:T(8,128)(2,1)}, bf16[512,1024]{1,0:T(8,128)(2,1)}, f32[8,128]{1,0:T(8,128)}) custom-call(bf16[16,16,1024]{2,1,0:T(8,128)(2,1)} %bitcast.7, bf16[8,512,1024]{2,1,0:T(8,128)(2,1)} %bitcast.6, bf16[16,16,1024]{2,1,0:T(8,128)(2,1)} %bitcast.8, f32[1,16]{1,0:T(1,128)} %ha.1, ...), custom_call_target="tpu_custom_call" | custom-call | tf_op jit(solution)/shard_map/pallas_call | solution.py:549
  146.7 3.8 %shard_map.110 = (bf16[16,16,1024]{2,1,0:T(8,128)(2,1)}, bf16[16,16,1024]{2,1,0:T(8,128)(2,1)}, bf16[512,1024]{1,0:T(8,128)(2,1)}, f32[1,16]{1,0:T(1,128)}, f32[1,16]{1,0:T(1,128)}, /*index=5*/f32[1,16]{1,0:T(1,128)}) custom-call(bf16[16,16,1024]{2,1,0:T(8,128)(2,1)} %get-tuple-element.16.a, bf16[16,16,1024]{2,1,0:T(8,128)(2,1)} %get-tuple-element.17.g, ...), custom_call_target="tpu_custom_call" | custom-call | tf_op jit(solution)/shard_map/pallas_call | solution.py:574

commit v4 on v3

--- a/solution.py
+++ b/solution.py
@@ -13,7 +13,7 @@
 BF16 = jnp.bfloat16
 CHUNK = 16
 AHEAD = 5
-WARM = 8
+WARM = 10
 
 scope = lambda name: contextlib.nullcontext()
 
@@ -30,11 +30,11 @@
     S, Z, T, n, R,
     acts, weights, cot, hist_act, hist_weight, hist_grad,
     out_acts, out_grads, out_wgrad, out_peaks,
-    w, wt, xg, xq, ar, gr, outv, gin, gout, gq, ps, pr, cotv, acc, wg, amax, wmax, gmax, pks, pky, pkm, pkz,
-    ld_w, ld_x, ld_c, st_o, st_g, st_w,
+    w, wt, xg, xq, ar, gr, outv, gin, gout, gq, ps, pr, cotv, acc, amax, wmax, gmax, pks, pky, pkm, pkz,
+    ld_w, ld_x, ld_c,
     f_recv, fg_send, fo_send, a_send, a_recv, ay_send, ay_recv, p_send, p_recv, go_send, go_recv,
     z_send, zr_recv, zo_recv,
-    ky_send, ky_recv, kz_send, kz_recv,
+    ky_send, ky_recv, kz_send, kz_recv, far, hist, ld_h,
 ):
     s = lax.axis_index("pipe")
     z = lax.axis_index("dp")
@@ -73,7 +73,7 @@
     barrier = pltpu.get_barrier_semaphore()
     for d in range(1, T):
         pl.semaphore_signal(barrier, inc=1, device_id={"tensor": at_y(d)}, device_id_type=MESH)
-    for d in range(1, Z):
+    for d in (1, Z - 1):
         pl.semaphore_signal(barrier, inc=1, device_id={"dp": at_z(d)}, device_id_type=MESH)
     for d in range(T):
         @pl.when(not_last)
@@ -89,17 +89,21 @@
     def load_w(r):
         return pltpu.make_async_copy(weights.at[r], w.at[r], ld_w.at[r])
 
-    def load_x(c, h):
-        return pltpu.make_async_copy(
-            acts.at[c, :, pl.ds(h * C, C)], xg.at[c, y * H + h], ld_x
-        )
+    def load_x(h):
+        return pltpu.make_async_copy(acts.at[:, :, pl.ds(h * C, C)], xg.at[:, y * H + h], ld_x)
 
     load_c = pltpu.make_async_copy(cot, cotv, ld_c)
+    load_h = [
+        pltpu.make_async_copy(old, hist.at[i], ld_h.at[i])
+        for i, old in enumerate((hist_act, hist_weight, hist_grad))
+    ]
+    for load in load_h:
+        load.start()
 
     @pl.when(first)
     def _():
         for h in range(H):
-            lax.fori_loop(0, n, lambda c, u: (load_x(c, h).start(), u)[1], 0)
+            load_x(h).start()
 
     lax.fori_loop(0, Z, lambda r, u: (load_w(r).start(), u)[1], 0)
 
@@ -107,9 +111,11 @@
     def _():
         load_c.start()
 
-    ha = jnp.max(hist_act[...], axis=1, keepdims=True)
-    hw = jnp.max(hist_weight[...], axis=1, keepdims=True)
-    hg = jnp.max(hist_grad[...], axis=1, keepdims=True)
+    for load in load_h:
+        load.wait()
+    ha = jnp.max(hist[0], axis=1, keepdims=True)
+    hw = jnp.max(hist[1], axis=1, keepdims=True)
+    hg = jnp.max(hist[2], axis=1, keepdims=True)
     act_factor = 448.0 / ha
     weight_factor = 448.0 / hw
     grad_factor = 57344.0 / hg
@@ -167,7 +173,7 @@
 
     with scope("barrier"):
         pairs = not_first.astype(jnp.int32) + not_last.astype(jnp.int32)
-        pl.semaphore_wait(barrier, (T - 1) + (Z - 1) + T * pairs)
+        pl.semaphore_wait(barrier, (T - 1) + 2 + T * pairs)
 
     def start_gather(c):
         for d in (2, 1, 3):
@@ -178,6 +184,12 @@
         for c in range(AHEAD):
             start_gather(c)
 
+    def far_signal(level):
+        for to in (level + 1, Z - 1 - level):
+            pl.semaphore_signal(far.at[level], inc=1, device_id={"dp": at_z(to)}, device_id_type=MESH)
+
+    far_signal(0)
+
     late = s >= S // 2
     early = jnp.logical_not(late)
 
@@ -186,8 +198,9 @@
         with scope("turn"):
             lax.fori_loop(0, T, turn_w, 0)
 
-    def store_out(c, h):
-        return pltpu.make_async_copy(outv.at[c, h], out_acts.at[c, :, pl.ds(h * C, C)], st_o)
+    with scope("far0"):
+        pl.semaphore_wait(far.at[0], 2)
+        far_signal(1)
 
     def forward(c, m):
         span = pl.ds(c, m)
@@ -231,6 +244,10 @@
                 def _():
                     start_gather(c + AHEAD)
 
+            @pl.when(c == 0)
+            def _():
+                pl.semaphore_wait(far.at[1], 2)
+
             @pl.when(c // Q == y)
             def _():
                 for d in (4, 3, 5, 2, 6, 1, 7):
@@ -238,8 +255,7 @@
                 ar[span, z] = xq[span, z]
 
             for h in range(H):
-                for i in range(m):
-                    store_out(c + i, h).start()
+                out_acts[span, :, h * C : (h + 1) * C] = outv[span, h]
                 x = xg[span, y * H + h].reshape(m * R, C).astype(F32)
                 amax[h] = jnp.maximum(amax[h], jnp.max(jnp.abs(x), axis=0, keepdims=True))
 
@@ -269,7 +285,19 @@
             recv = zo_recv.at[u]
         return rcopy(ref, ref, z_send, recv, dp=at_z(Z - 1 if back else 1))
 
-    lag = jnp.where(s < 2, 1, 2)
+    lag = jnp.where(s < 2, 1, jnp.where(s < S - 2, 3, 4))
+
+    def skip_copy(u, back):
+        span = pl.ds(2 * u, 2)
+        return rcopy(gq.at[span], gr.at[span, z], z_send, zr_recv.at[u, 3 * back + 1], dp=at_z(Z - 2 if back else 2))
+
+    def over_copy(u, back):
+        half = H * C // 2
+        ref = gr.at[pl.ds(2 * u, 2), at_z(2 if back else Z - 2), :, pl.ds(half * back, half)]
+        return rcopy(ref, ref, z_send, zo_recv.at[u], dp=at_z(Z - 2 if back else 2))
+
+    def short(u):
+        return first & (u == U - 1)
 
     def relays(t):
         for level in (1, 2, 3):
@@ -281,10 +309,16 @@
                     for back in (0, 1):
                         k = at_z(level if back else Z - level)
                         drain_recv(zr_recv.at[u, 3 * back + level - 1], gr.at[pl.ds(2 * u, 2), k])
-                        relay_copy(u, level, back).start()
-
-    def store_g(c):
-        return pltpu.make_async_copy(gout.at[c], out_grads.at[c], st_g)
+                        if level == 2:
+                            relay_copy(u, level, back).start()
+
+                            @pl.when(short(u))
+                            def _():
+                                over_copy(u, back).start()
+                        else:
+                            @pl.when(jnp.logical_not(short(u)))
+                            def _():
+                                relay_copy(u, level, back).start()
 
     @pl.when(last)
     def _():
@@ -380,6 +414,11 @@
 
         @pl.when(bwd_pair | (bwd_one & (lax.rem(late_k, 2) == 1)))
         def _():
+            @pl.when(short(unit))
+            def _():
+                skip_copy(unit, 0).start()
+                skip_copy(unit, 1).start()
+
             ring_copy(unit, 0).start()
             ring_copy(unit, 1).start()
             relays(unit)
@@ -411,6 +450,17 @@
     for d in range(1, T):
         ky_copy(d).start()
 
+    def over_tensor():
+        with scope("kwait"):
+            drain_recv(ky_recv, pky.at[pl.ds(0, T - 1)])
+        pky[y] = pks[...]
+        most = pky[0]
+        for k in range(1, T):
+            most = jnp.maximum(most, pky[k])
+        pkm[...] = most
+        for d in range(1, Z):
+            kz_copy(d).start()
+
     def rows_product(lo, count):
         left = ar[lo : lo + count].reshape(count * Z * R, C)
         right = gr[lo : lo + count].reshape(count * Z * R, H * C)
@@ -426,29 +476,33 @@
             wait_opposite(0, U // 2)
             acc[...] = rows_product(0, n // 2)
 
+    def next_rows():
+        with scope("wgrad2"):
+            wait_opposite(U // 2, U - 2)
+            acc[...] += rows_product(n // 2, n // 2 - 4)
+
+    near = s < 2
+
     def rest(k, u):
+        pl.when(early & (k == jnp.where(near, U, U + 5)))(first_rows)
+        pl.when(near & (k == U + 2))(next_rows)
         relays(k)
-
-        @pl.when(late & (k == U + 1))
+        pl.when(k == U + 1)(over_tensor)
+
+        @pl.when(late & (k == U + 2))
         def _():
             share_acts()
 
-        @pl.when(early & (k == U - 1 + lag))
-        def _():
-            first_rows()
-
         return u
 
+    yields = is_odd & (s > 1)
+
+    @pl.when(yields)
+    def _():
+        with scope("yield"):
+            drain_recv(go_recv, gout)
+
     lax.fori_loop(U, U + 3 * lag, rest, 0)
-
-    with scope("kwait"):
-        drain_recv(ky_recv, pky.at[pl.ds(0, T - 1)])
-    pky[y] = tile
-    for k in range(T):
-        tile = jnp.maximum(tile, pky[k])
-    pkm[...] = tile
-    for d in range(1, Z):
-        kz_copy(d).start()
 
     @pl.when(first)
     def _():
@@ -464,29 +518,26 @@
             drain_recv(p_recv.at[n], pr.at[1, :, pl.ds(0, T - 1)])
             lax.fori_loop(0, n, finish, 0)
 
-    @pl.when(not_first)
+    @pl.when(not_first & jnp.logical_not(yields))
     def _():
         with scope("backwait"):
             drain_recv(go_recv, gout)
 
-    lax.fori_loop(0, n, lambda c, u: (store_g(c).start(), u)[1], 0)
+    out_grads[...] = gout[...]
 
     pl.when(late)(first_rows)
-    with scope("wgrad2"):
-        wait_opposite(U // 2, U - 1)
-        acc[...] += rows_product(n // 2, n // 2 - 2)
+    pl.when(jnp.logical_not(near))(next_rows)
     with scope("zwait_last"):
-        wait_opposite(U - 1, U)
+        wait_opposite(U - 2, U)
     with scope("wgrad_last"):
-        wg[...] = ((acc[...] + rows_product(n - 2, 2)) * update_factor).astype(BF16)
-    st = pltpu.make_async_copy(wg, out_wgrad, st_w)
-    st.start()
+        out_wgrad[...] = ((acc[...] + rows_product(n - 4, 4)) * update_factor).astype(BF16)
 
     drain_recv(kz_recv, pkz.at[pl.ds(0, Z - 1)])
-    pkz[z] = tile
-    for k in range(Z):
-        tile = jnp.maximum(tile, pkz[k])
-    out_peaks[...] = tile
+    pkz[z] = pkm[...]
+    most = pkz[0]
+    for k in range(1, Z):
+        most = jnp.maximum(most, pkz[k])
+    out_peaks[...] = most
 
     with scope("close"):
         drain_send(ky_send, pky.at[pl.ds(0, T - 1)])
@@ -509,22 +560,14 @@
             drain_send(fo_send, pr.at[0])
             drain_send(go_send, gin)
 
-        pltpu.make_async_copy(outv, outv, st_o).wait()
-        pltpu.make_async_copy(gout, gout, st_g).wait()
-        st.wait()
-
-
-def finish_kernel(a, g, m, peaks, ha, hw, hg, oa, og, om, na, nw, ng, va, vg, vm, load, store):
-    loads = [pltpu.make_async_copy(x, v, load.at[i]) for i, (x, v) in enumerate(((a, va), (g, vg), (m, vm)))]
-    stores = [pltpu.make_async_copy(v, o, store.at[i]) for i, (v, o) in enumerate(((va, oa), (vg, og), (vm, om)))]
-    for c in loads:
-        c.start()
+
+def finish_kernel(a, g, m, peaks, ha, hw, hg, oa, og, om, na, nw, ng, store):
+    stores = [pltpu.make_async_copy(v, o, store.at[i]) for i, (v, o) in enumerate(((a, oa), (g, og), (m, om)))]
+    for d in stores:
+        d.start()
     for i, (old, new) in enumerate(((ha, na), (hw, nw), (hg, ng))):
         new[:, 1:] = old[:, :-1]
         new[:, 0:1] = peaks[i : i + 1, 0:1]
-    for c, d in zip(loads, stores):
-        c.wait()
-        d.start()
     for d in stores:
         d.wait()
 
@@ -537,8 +580,8 @@
     n = micro * rows // R
     H = Z // T
     C = depth // Z
-    acts = acts_in.reshape(n, R, width)
-    cot = cotangent.reshape(n, R, width)
+    acts = pltpu.with_memory_space_constraint(acts_in.reshape(n, R, width), pltpu.HBM)
+    cot = pltpu.with_memory_space_constraint(cotangent.reshape(n, R, width), pltpu.HBM)
     w = weights.reshape(Z, C, width)
     any_ = pl.BlockSpec(memory_space=pl.ANY)
     hbm = pl.BlockSpec(memory_space=pltpu.HBM)
@@ -554,22 +597,22 @@
             jax.ShapeDtypeStruct((C, width), BF16),
             jax.ShapeDtypeStruct((8, 128), F32),
         ),
-        in_specs=[any_, any_, any_, vmem, vmem, vmem],
-        out_specs=(any_, any_, any_, vmem),
+        in_specs=[any_] * 6,
+        out_specs=(vmem, vmem, vmem, vmem),
         scratch_shapes=[
             b(Z, C, width), b(T, width, width), b(n, Z, R, C), b(n, Z, R, C), b(n, Z, R, C), b(n, Z, R, width),
             b(n, H, R, C), b(n, R, width), b(n, R, width), b(n, R, width),
             b(n, T, H, R, C), b(2, n, T, H, R, C), b(n, R, width), f(C, width),
-            b(C, width), f(H, 1, C), f(1, width), f(1, width),
+            f(H, 1, C), f(1, width), f(1, width),
             f(8, 128), f(T, 8, 128), f(8, 128), f(Z, 8, 128),
-            dma((Z,)), *(dma,) * 5,
+            dma((Z,)), dma, dma,
             dma((n, T)), *(dma,) * 7, dma((n + 1,)), dma, dma, dma, dma((n // 2, 6)), dma((n // 2,)),
-            *(dma,) * 4,
+            *(dma,) * 4, pltpu.SemaphoreType.REGULAR((2,)), f(3, *hist_act.shape), dma((3,)),
         ],
         compiler_params=pltpu.CompilerParams(
-            collective_id=0, has_side_effects=True, vmem_limit_bytes=60 * 1024 * 1024
+            collective_id=0, has_side_effects=True, vmem_limit_bytes=52000000
         ),
-    )(acts, w, cot, hist_act, hist_weight, hist_grad)
+    )(acts, w, cot, *(pltpu.with_memory_space_constraint(h, pltpu.HBM) for h in (hist_act, hist_weight, hist_grad)))
 
     final = pl.pallas_call(
         finish_kernel,
@@ -579,10 +622,10 @@
             jax.ShapeDtypeStruct((C, width), BF16),
             *(jax.ShapeDtypeStruct(hist_act.shape, F32) for _ in range(3)),
         ),
-        in_specs=[hbm, hbm, hbm, vmem, vmem, vmem, vmem],
+        in_specs=[vmem] * 7,
         out_specs=(hbm, hbm, hbm, vmem, vmem, vmem),
-        scratch_shapes=[b(n, R, width), b(n, R, width), b(C, width), dma((3,)), dma((3,))],
-        compiler_params=pltpu.CompilerParams(vmem_limit_bytes=60 * 1024 * 1024),
+        scratch_shapes=[dma((3,))],
+        compiler_params=pltpu.CompilerParams(vmem_limit_bytes=8 * 1024 * 1024),
     )(out_acts, out_grads, out_w, peaks, hist_act, hist_weight, hist_grad)
     return (
         final[0].reshape(1, micro, rows, width),

time: 151 us -> 149 us (0.987)
  Pallas kernels: 150 us -> 148 us
    pallas_call x1, Pallas kernels: 3.79 us -> 1.86 us  [step(): pl.pallas_call(finish_kernel, out_shape=(jax.ShapeDtypeStruct((n, R, widt...]
where the time goes in v4:
time: 149 us; the launch traced here: 148 us
  Pallas kernels  148 us (99%)
    pallas_call x1, Pallas kernels, step(): pl.pallas_call(functools.partial(kernel, S, Z, T, n, R), out_shape=(jax.S...  146 us

profile of v4, /device:TPU:32, one launch (start us, length us, event | category | flops | bytes accessed | tf_op | source)
XLA Modules:
  0.0 148.5 jit_solution(5397811100851149203)
XLA Ops:
  0.6 0.0 copy-start.2
  0.6 0.0 copy-start.1
  0.7 0.0 copy-start
  0.7 145.9 %shard_map.109 = (bf16[16,16,1024]{2,1,0:T(8,128)(2,1)S(1)}, bf16[16,16,1024]{2,1,0:T(8,128)(2,1)S(1)}, bf16[512,1024]{1,0:T(8,128)(2,1)S(1)}, f32[8,128]{1,0:T(8,128)S(1)}) custom-call(bf16[16,16,1024]{2,1,0:T(8,128)(2,1)} %bitcast.7, bf16[8,512,1024]{2,1,0:T(8,128)(2,1)} %bitcast.6, bf16[16,16,1024]{2,1,0:T(8,128)(2,1)} %bitcast.8, f32[1,16]{1,0:T(1,128)} %ha.1, ...), custom_call_target="tpu_custom_call" | custom-call | tf_op jit(solution)/shard_map/pallas_call | solution.py:592
  146.6 0.0 copy-done.2
  146.6 0.0 copy-done.1
  146.6 0.0 copy-done
  146.6 1.9 %shard_map.110 = (bf16[16,16,1024]{2,1,0:T(8,128)(2,1)}, bf16[16,16,1024]{2,1,0:T(8,128)(2,1)}, bf16[512,1024]{1,0:T(8,128)(2,1)}, f32[1,16]{1,0:T(1,128)}, f32[1,16]{1,0:T(1,128)}, /*index=5*/f32[1,16]{1,0:T(1,128)}) custom-call(bf16[16,16,1024]{2,1,0:T(8,128)(2,1)S(1)} %get-tuple-element.16.a, bf16[16,16,1024]{2,1,0:T(8,128)(2,1)S(1)} %get-tuple-element.17.g, ...), custom_call_target="tpu_custom_call" | custom-call | tf_op jit(solution)/shard_map/pallas_call | solution.py:617
Async XLA Ops:
  0.6 145.9 %copy-start.2 = (f32[1,16]{1,0:T(1,128)S(1)}, f32[1,16]{1,0:T(1,128)}, u32[]{:S(2)}) copy-start(f32[1,16]{1,0:T(1,128)} %hg.1) | copy-start | bytes 196
  0.6 145.9 %copy-start.1 = (f32[1,16]{1,0:T(1,128)S(1)}, f32[1,16]{1,0:T(1,128)}, u32[]{:S(2)}) copy-start(f32[1,16]{1,0:T(1,128)} %hw.1) | copy-start | bytes 196
  0.7 145.9 %copy-start = (f32[1,16]{1,0:T(1,128)S(1)}, f32[1,16]{1,0:T(1,128)}, u32[]{:S(2)}) copy-start(f32[1,16]{1,0:T(1,128)} %ha.1) | copy-start | bytes 196

commit v5 on v4

--- a/solution.py
+++ b/solution.py
@@ -14,6 +14,7 @@
 CHUNK = 16
 AHEAD = 5
 WARM = 10
+LENT = 2
 
 scope = lambda name: contextlib.nullcontext()
 
@@ -30,10 +31,11 @@
     S, Z, T, n, R,
     acts, weights, cot, hist_act, hist_weight, hist_grad,
     out_acts, out_grads, out_wgrad, out_peaks,
-    w, wt, xg, xq, ar, gr, outv, gin, gout, gq, ps, pr, cotv, acc, amax, wmax, gmax, pks, pky, pkm, pkz,
+    w, wt, xg, xq, ar, gr, outv, gin, gout, gq, ps, pr, cotv, hb, acc, amax, wmax, gmax, pks, pky, pkm, pkz,
     ld_w, ld_x, ld_c,
     f_recv, fg_send, fo_send, a_send, a_recv, ay_send, ay_recv, p_send, p_recv, go_send, go_recv,
     z_send, zr_recv, zo_recv,
+    h_send, h_recv, hz_send, hr_recv, ho_recv, hx_send, hx_recv,
     ky_send, ky_recv, kz_send, kz_recv, far, hist, ld_h,
 ):
     s = lax.axis_index("pipe")
@@ -49,6 +51,9 @@
     first = s == 0
     last = s == S - 1
     not_last = jnp.logical_not(last)
+    near = s < 2
+    helper = s >= S - 2
+    buddy = jnp.where(near, s + S - 2, jnp.maximum(s - (S - 2), 0))
     not_first = jnp.logical_not(first)
     up = jnp.minimum(s + 1, S - 1)
     down = jnp.maximum(s - 1, 0)
@@ -83,6 +88,10 @@
         @pl.when(not_first)
         def _():
             pl.semaphore_signal(barrier, inc=1, device_id={"pipe": down, "tensor": at_y(d)}, device_id_type=MESH)
+
+    @pl.when(near | helper)
+    def _():
+        pl.semaphore_signal(barrier, inc=1, device_id={"pipe": buddy}, device_id_type=MESH)
 
     own = pl.ds(y * H, H)
 
@@ -146,15 +155,16 @@
         span = pl.ds(c, m)
         return rcopy(xq.at[span, r], ar.at[span, z], a_send, a_recv, dp=r)
 
-    def share_copy(d):
-        span = pl.ds(y * Q, Q)
+    def share_copy(d, j):
+        span = pl.ds(2 * (y + T * j), 2)
         return rcopy(ar.at[span], ar.at[span], ay_send, ay_recv, tensor=at_y(d))
 
     def share_acts():
         with scope("share"):
             drain_recv(a_recv, ar.at[pl.ds(0, Q), pl.ds(0, Z - 1)])
-            for d in (2, 1, 3):
-                share_copy(d).start()
+            for j in range(U // T):
+                for d in (2, 1, 3):
+                    share_copy(d, j).start()
 
     def quant_w(r, u):
         load_w(r).wait()
@@ -173,7 +183,7 @@
 
     with scope("barrier"):
         pairs = not_first.astype(jnp.int32) + not_last.astype(jnp.int32)
-        pl.semaphore_wait(barrier, (T - 1) + 2 + T * pairs)
+        pl.semaphore_wait(barrier, (T - 1) + 2 + T * pairs + (near | helper).astype(jnp.int32))
 
     def start_gather(c):
         for d in (2, 1, 3):
@@ -248,7 +258,7 @@
             def _():
                 pl.semaphore_wait(far.at[1], 2)
 
-            @pl.when(c // Q == y)
+            @pl.when(lax.rem(c // 2, T) == y)
             def _():
                 for d in (4, 3, 5, 2, 6, 1, 7):
                     act_copy(c, m, d).start()
@@ -285,7 +295,7 @@
             recv = zo_recv.at[u]
         return rcopy(ref, ref, z_send, recv, dp=at_z(Z - 1 if back else 1))
 
-    lag = jnp.where(s < 2, 1, jnp.where(s < S - 2, 3, 4))
+    lag = jnp.where(s < 2, 1, 3)
 
     def skip_copy(u, back):
         span = pl.ds(2 * u, 2)
@@ -296,6 +306,50 @@
         ref = gr.at[pl.ds(2 * u, 2), at_z(2 if back else Z - 2), :, pl.ds(half * back, half)]
         return rcopy(ref, ref, z_send, zo_recv.at[u], dp=at_z(Z - 2 if back else 2))
 
+    def lent(u):
+        return near & (lax.rem(u, 2) == 1) & (u < 2 * LENT)
+
+    def lend_copy(u):
+        i = u // 2
+        return rcopy(gq.at[pl.ds(2 * u, 2)], hb.at[pl.ds(2 * i, 2), z], h_send, h_recv.at[i], pipe=buddy)
+
+    def help_copy(i, level, back):
+        span = pl.ds(2 * i, 2)
+        k = at_z(level if back else Z - level) if level else z
+        if level < 3:
+            ref, recv = hb.at[span, k], hr_recv.at[i, 3 * back + level]
+        else:
+            half = H * C // 2
+            ref, recv = hb.at[span, k, :, pl.ds(half * back, half)], ho_recv.at[i]
+        return rcopy(ref, ref, hz_send, recv, dp=at_z(Z - 1 if back else 1))
+
+    def return_copy(i, k):
+        return rcopy(hb.at[pl.ds(2 * i, 2), k], gr.at[pl.ds(4 * i + 2, 2), k], hx_send, hx_recv.at[i], pipe=buddy)
+
+    def assist(t, v):
+        for level in range(5):
+            i = t - level
+
+            @pl.when((i >= 0) & (i < LENT))
+            def _():
+                span = pl.ds(2 * i, 2)
+                with scope(f"assist{level}"):
+                    if level == 0:
+                        drain_recv(h_recv.at[i], hb.at[span, z])
+                        help_copy(i, 0, 0).start()
+                        help_copy(i, 0, 1).start()
+                    elif level < 4:
+                        for back in (0, 1):
+                            k = at_z(level if back else Z - level)
+                            drain_recv(hr_recv.at[i, 3 * back + level - 1], hb.at[span, k])
+                            help_copy(i, level, back).start()
+                            return_copy(i, k).start()
+                    else:
+                        drain_recv(ho_recv.at[i], hb.at[span, at_z(4)])
+                        return_copy(i, at_z(4)).start()
+
+        return v
+
     def short(u):
         return first & (u == U - 1)
 
@@ -303,7 +357,7 @@
         for level in (1, 2, 3):
             u = t - lag * level
 
-            @pl.when((u >= 0) & (u < U))
+            @pl.when((u >= 0) & (u < U) & jnp.logical_not(lent(u)))
             def _():
                 with scope(f"relay{level}"):
                     for back in (0, 1):
@@ -419,8 +473,15 @@
                 skip_copy(unit, 0).start()
                 skip_copy(unit, 1).start()
 
-            ring_copy(unit, 0).start()
-            ring_copy(unit, 1).start()
+            @pl.when(lent(unit))
+            def _():
+                lend_copy(unit).start()
+
+            @pl.when(jnp.logical_not(lent(unit)))
+            def _():
+                ring_copy(unit, 0).start()
+                ring_copy(unit, 1).start()
+
             relays(unit)
 
         @pl.when(early & (k == n - 1))
@@ -468,7 +529,17 @@
 
     def wait_opposite(lo, hi):
         for u in range(lo, hi):
-            drain_recv(zo_recv.at[u], gr.at[pl.ds(2 * u, 2), 0])
+            def own_ring():
+                drain_recv(zo_recv.at[u], gr.at[pl.ds(2 * u, 2), 0])
+
+            if u % 2 == 1 and u < 2 * LENT:
+                @pl.when(near)
+                def _():
+                    drain_recv(hx_recv.at[u // 2], gr.at[pl.ds(2 * u, 2), pl.ds(0, Z - 1)])
+
+                pl.when(jnp.logical_not(near))(own_ring)
+            else:
+                own_ring()
 
     def first_rows():
         with scope("wgrad"):
@@ -481,13 +552,10 @@
             wait_opposite(U // 2, U - 2)
             acc[...] += rows_product(n // 2, n // 2 - 4)
 
-    near = s < 2
-
     def rest(k, u):
-        pl.when(early & (k == jnp.where(near, U, U + 5)))(first_rows)
-        pl.when(near & (k == U + 2))(next_rows)
+        pl.when(near & (k == U + 2))(first_rows)
         relays(k)
-        pl.when(k == U + 1)(over_tensor)
+        pl.when(k == U)(over_tensor)
 
         @pl.when(late & (k == U + 2))
         def _():
@@ -503,6 +571,10 @@
             drain_recv(go_recv, gout)
 
     lax.fori_loop(U, U + 3 * lag, rest, 0)
+
+    @pl.when(helper)
+    def _():
+        lax.fori_loop(0, LENT + 4, assist, 0)
 
     @pl.when(first)
     def _():
@@ -525,8 +597,8 @@
 
     out_grads[...] = gout[...]
 
-    pl.when(late)(first_rows)
-    pl.when(jnp.logical_not(near))(next_rows)
+    pl.when(jnp.logical_not(near))(first_rows)
+    next_rows()
     with scope("zwait_last"):
         wait_opposite(U - 2, U)
     with scope("wgrad_last"):
@@ -544,7 +616,20 @@
         drain_send(kz_send, pkz.at[pl.ds(0, Z - 1)])
         drain_send(a_send, ar.at[pl.ds(0, Q), pl.ds(0, Z - 1)])
         drain_send(ay_send, ar.at[pl.ds(0, (T - 1) * Q)])
-        drain_send(z_send, gr.at[:, pl.ds(0, Z - 1)])
+        @pl.when(near)
+        def _():
+            drain_send(z_send, gr.at[pl.ds(0, n - 2 * LENT), pl.ds(0, Z - 1)])
+            drain_send(h_send, hb.at[:, 0])
+
+        @pl.when(jnp.logical_not(near))
+        def _():
+            drain_send(z_send, gr.at[:, pl.ds(0, Z - 1)])
+
+        @pl.when(helper)
+        def _():
+            drain_send(hz_send, hb.at[:, pl.ds(0, Z - 1)])
+            drain_send(hx_send, hb.at[:, pl.ds(0, Z - 1)])
+
 
         @pl.when(first)
         def _():
@@ -602,11 +687,12 @@
         scratch_shapes=[
             b(Z, C, width), b(T, width, width), b(n, Z, R, C), b(n, Z, R, C), b(n, Z, R, C), b(n, Z, R, width),
             b(n, H, R, C), b(n, R, width), b(n, R, width), b(n, R, width),
-            b(n, T, H, R, C), b(2, n, T, H, R, C), b(n, R, width), f(C, width),
+            b(n, T, H, R, C), b(2, n, T, H, R, C), b(n, R, width), b(2 * LENT, Z, R, width), f(C, width),
             f(H, 1, C), f(1, width), f(1, width),
             f(8, 128), f(T, 8, 128), f(8, 128), f(Z, 8, 128),
             dma((Z,)), dma, dma,
             dma((n, T)), *(dma,) * 7, dma((n + 1,)), dma, dma, dma, dma((n // 2, 6)), dma((n // 2,)),
+            dma, dma((LENT,)), dma, dma((LENT, 6)), dma((LENT,)), dma, dma((LENT,)),
             *(dma,) * 4, pltpu.SemaphoreType.REGULAR((2,)), f(3, *hist_act.shape), dma((3,)),
         ],
         compiler_params=pltpu.CompilerParams(

time: 149 us -> 143 us (0.960)
  Pallas kernels: 148 us -> 142 us
    pallas_call x1, Pallas kernels: 146 us -> 140 us  [step(): pl.pallas_call(functools.partial(kernel, S, Z, T, n, R), out_shape=(jax.S...]
where the time goes in v5:
time: 143 us; the launch traced here: 142 us
  Pallas kernels  142 us (99%)
    pallas_call x1, Pallas kernels, step(): pl.pallas_call(functools.partial(kernel, S, Z, T, n, R), out_shape=(jax.S...  140 us

profile of v5, /device:TPU:32, one launch (start us, length us, event | category | flops | bytes accessed | tf_op | source)
XLA Modules:
  0.0 142.4 jit_solution(13303156795873019288)
XLA Ops:
  0.6 0.0 copy-start.2
  0.6 0.0 copy-start.1
  0.7 0.0 copy-start
  0.7 139.9 %shard_map.109 = (bf16[16,16,1024]{2,1,0:T(8,128)(2,1)S(1)}, bf16[16,16,1024]{2,1,0:T(8,128)(2,1)S(1)}, bf16[512,1024]{1,0:T(8,128)(2,1)S(1)}, f32[8,128]{1,0:T(8,128)S(1)}) custom-call(bf16[16,16,1024]{2,1,0:T(8,128)(2,1)} %bitcast.7, bf16[8,512,1024]{2,1,0:T(8,128)(2,1)} %bitcast.6, bf16[16,16,1024]{2,1,0:T(8,128)(2,1)} %bitcast.8, f32[1,16]{1,0:T(1,128)} %ha.1, ...), custom_call_target="tpu_custom_call" | custom-call | tf_op jit(solution)/shard_map/pallas_call | solution.py:677
  140.5 0.0 copy-done.2
  140.6 0.0 copy-done.1
  140.6 0.0 copy-done
  140.6 1.9 %shard_map.110 = (bf16[16,16,1024]{2,1,0:T(8,128)(2,1)}, bf16[16,16,1024]{2,1,0:T(8,128)(2,1)}, bf16[512,1024]{1,0:T(8,128)(2,1)}, f32[1,16]{1,0:T(1,128)}, f32[1,16]{1,0:T(1,128)}, /*index=5*/f32[1,16]{1,0:T(1,128)}) custom-call(bf16[16,16,1024]{2,1,0:T(8,128)(2,1)S(1)} %get-tuple-element.16.a, bf16[16,16,1024]{2,1,0:T(8,128)(2,1)S(1)} %get-tuple-element.17.g, ...), custom_call_target="tpu_custom_call" | custom-call | tf_op jit(solution)/shard_map/pallas_call | solution.py:703
Async XLA Ops:
  0.6 139.9 %copy-start.2 = (f32[1,16]{1,0:T(1,128)S(1)}, f32[1,16]{1,0:T(1,128)}, u32[]{:S(2)}) copy-start(f32[1,16]{1,0:T(1,128)} %hg.1) | copy-start | bytes 196
  0.6 139.9 %copy-start.1 = (f32[1,16]{1,0:T(1,128)S(1)}, f32[1,16]{1,0:T(1,128)}, u32[]{:S(2)}) copy-start(f32[1,16]{1,0:T(1,128)} %hw.1) | copy-start | bytes 196
  0.7 139.9 %copy-start = (f32[1,16]{1,0:T(1,128)S(1)}, f32[1,16]{1,0:T(1,128)}, u32[]{:S(2)}) copy-start(f32[1,16]{1,0:T(1,128)} %ha.1) | copy-start | bytes 196

commit v6 on v5

--- a/solution.py
+++ b/solution.py
@@ -53,6 +53,8 @@
     not_last = jnp.logical_not(last)
     near = s < 2
     helper = s >= S - 2
+    most_lent = first | (s == S - 2)
+    loans = jnp.where(most_lent, LENT, LENT - 1)
     buddy = jnp.where(near, s + S - 2, jnp.maximum(s - (S - 2), 0))
     not_first = jnp.logical_not(first)
     up = jnp.minimum(s + 1, S - 1)
@@ -307,7 +309,7 @@
         return rcopy(ref, ref, z_send, zo_recv.at[u], dp=at_z(Z - 2 if back else 2))
 
     def lent(u):
-        return near & (lax.rem(u, 2) == 1) & (u < 2 * LENT)
+        return near & (lax.rem(u, 2) == 1) & (u < 2 * loans)
 
     def lend_copy(u):
         i = u // 2
@@ -330,7 +332,7 @@
         for level in range(5):
             i = t - level
 
-            @pl.when((i >= 0) & (i < LENT))
+            @pl.when((i >= 0) & (i < loans))
             def _():
                 span = pl.ds(2 * i, 2)
                 with scope(f"assist{level}"):
@@ -353,8 +355,8 @@
     def short(u):
         return first & (u == U - 1)
 
-    def relays(t):
-        for level in (1, 2, 3):
+    def relays(t, levels=(1, 2, 3)):
+        for level in levels:
             u = t - lag * level
 
             @pl.when((u >= 0) & (u < U) & jnp.logical_not(lent(u)))
@@ -533,11 +535,13 @@
                 drain_recv(zo_recv.at[u], gr.at[pl.ds(2 * u, 2), 0])
 
             if u % 2 == 1 and u < 2 * LENT:
-                @pl.when(near)
+                by_helper = near if u < 2 * LENT - 2 else first
+
+                @pl.when(by_helper)
                 def _():
                     drain_recv(hx_recv.at[u // 2], gr.at[pl.ds(2 * u, 2), pl.ds(0, Z - 1)])
 
-                pl.when(jnp.logical_not(near))(own_ring)
+                pl.when(jnp.logical_not(by_helper))(own_ring)
             else:
                 own_ring()
 
@@ -552,32 +556,7 @@
             wait_opposite(U // 2, U - 2)
             acc[...] += rows_product(n // 2, n // 2 - 4)
 
-    def rest(k, u):
-        pl.when(near & (k == U + 2))(first_rows)
-        relays(k)
-        pl.when(k == U)(over_tensor)
-
-        @pl.when(late & (k == U + 2))
-        def _():
-            share_acts()
-
-        return u
-
-    yields = is_odd & (s > 1)
-
-    @pl.when(yields)
-    def _():
-        with scope("yield"):
-            drain_recv(go_recv, gout)
-
-    lax.fori_loop(U, U + 3 * lag, rest, 0)
-
-    @pl.when(helper)
-    def _():
-        lax.fori_loop(0, LENT + 4, assist, 0)
-
-    @pl.when(first)
-    def _():
+    def own_grads():
         def finish(c, u):
             for h in range(H):
                 g = ps[c, y, h].astype(F32)
@@ -590,6 +569,36 @@
             drain_recv(p_recv.at[n], pr.at[1, :, pl.ds(0, T - 1)])
             lax.fori_loop(0, n, finish, 0)
 
+    def rest(k, u):
+        @pl.when(first & (k == U + 2))
+        def _():
+            own_grads()
+            next_rows()
+
+        relays(k, (1, 2))
+        pl.when(first & (k == U + 1))(first_rows)
+        relays(k, (3,))
+        pl.when(k == U)(over_tensor)
+
+        @pl.when(late & (k == U + 2))
+        def _():
+            share_acts()
+
+        return u
+
+    yields = is_odd & (s > 1)
+
+    @pl.when(yields)
+    def _():
+        with scope("yield"):
+            drain_recv(go_recv, gout)
+
+    lax.fori_loop(U, U + 3 * lag, rest, 0)
+
+    @pl.when(helper)
+    def _():
+        lax.fori_loop(0, loans + 4, assist, 0)
+
     @pl.when(not_first & jnp.logical_not(yields))
     def _():
         with scope("backwait"):
@@ -597,8 +606,11 @@
 
     out_grads[...] = gout[...]
 
-    pl.when(jnp.logical_not(near))(first_rows)
-    next_rows()
+    @pl.when(not_first)
+    def _():
+        first_rows()
+        next_rows()
+
     with scope("zwait_last"):
         wait_opposite(U - 2, U)
     with scope("wgrad_last"):
@@ -616,19 +628,20 @@
         drain_send(kz_send, pkz.at[pl.ds(0, Z - 1)])
         drain_send(a_send, ar.at[pl.ds(0, Q), pl.ds(0, Z - 1)])
         drain_send(ay_send, ar.at[pl.ds(0, (T - 1) * Q)])
-        @pl.when(near)
-        def _():
-            drain_send(z_send, gr.at[pl.ds(0, n - 2 * LENT), pl.ds(0, Z - 1)])
-            drain_send(h_send, hb.at[:, 0])
+        for who, count in ((most_lent, LENT), (jnp.logical_not(most_lent), LENT - 1)):
+            @pl.when(near & who)
+            def _():
+                drain_send(z_send, gr.at[pl.ds(0, n - 2 * count), pl.ds(0, Z - 1)])
+                drain_send(h_send, hb.at[pl.ds(0, 2 * count), 0])
+
+            @pl.when(helper & who)
+            def _():
+                drain_send(hz_send, hb.at[pl.ds(0, 2 * count), pl.ds(0, Z - 1)])
+                drain_send(hx_send, hb.at[pl.ds(0, 2 * count), pl.ds(0, Z - 1)])
 
         @pl.when(jnp.logical_not(near))
         def _():
             drain_send(z_send, gr.at[:, pl.ds(0, Z - 1)])
-
-        @pl.when(helper)
-        def _():
-            drain_send(hz_send, hb.at[:, pl.ds(0, Z - 1)])
-            drain_send(hx_send, hb.at[:, pl.ds(0, Z - 1)])
 
 
         @pl.when(first)

time: 143 us -> 143 us (level)
  no operation moved by 1% of the time
where the time goes in v6:
time: 143 us
  Pallas kernels  143 us (100%)
    pallas_call x1, Pallas kernels, step(): pl.pallas_call(functools.partial(kernel, S, Z, T, n, R), out_shape=(jax.S...  141 us

profile of v6, /device:TPU:32, one launch (start us, length us, event | category | flops | bytes accessed | tf_op | source)
XLA Modules:
  0.0 143.4 jit_solution(18336989660663660141)
XLA Ops:
  0.6 0.0 copy-start.2
  0.6 0.0 copy-start.1
  0.7 0.0 copy-start
  0.7 140.8 %shard_map.109 = (bf16[16,16,1024]{2,1,0:T(8,128)(2,1)S(1)}, bf16[16,16,1024]{2,1,0:T(8,128)(2,1)S(1)}, bf16[512,1024]{1,0:T(8,128)(2,1)S(1)}, f32[8,128]{1,0:T(8,128)S(1)}) custom-call(bf16[16,16,1024]{2,1,0:T(8,128)(2,1)} %bitcast.7, bf16[8,512,1024]{2,1,0:T(8,128)(2,1)} %bitcast.6, bf16[16,16,1024]{2,1,0:T(8,128)(2,1)} %bitcast.8, f32[1,16]{1,0:T(1,128)} %ha.1, ...), custom_call_target="tpu_custom_call" | custom-call | tf_op jit(solution)/shard_map/pallas_call | solution.py:690
  141.5 0.0 copy-done.2
  141.5 0.0 copy-done.1
  141.5 0.0 copy-done
  141.5 1.9 %shard_map.110 = (bf16[16,16,1024]{2,1,0:T(8,128)(2,1)}, bf16[16,16,1024]{2,1,0:T(8,128)(2,1)}, bf16[512,1024]{1,0:T(8,128)(2,1)}, f32[1,16]{1,0:T(1,128)}, f32[1,16]{1,0:T(1,128)}, /*index=5*/f32[1,16]{1,0:T(1,128)}) custom-call(bf16[16,16,1024]{2,1,0:T(8,128)(2,1)S(1)} %get-tuple-element.16.a, bf16[16,16,1024]{2,1,0:T(8,128)(2,1)S(1)} %get-tuple-element.17.g, ...), custom_call_target="tpu_custom_call" | custom-call | tf_op jit(solution)/shard_map/pallas_call | solution.py:716
Async XLA Ops:
  0.6 140.9 %copy-start.2 = (f32[1,16]{1,0:T(1,128)S(1)}, f32[1,16]{1,0:T(1,128)}, u32[]{:S(2)}) copy-start(f32[1,16]{1,0:T(1,128)} %hg.1) | copy-start | bytes 196
  0.6 140.9 %copy-start.1 = (f32[1,16]{1,0:T(1,128)S(1)}, f32[1,16]{1,0:T(1,128)}, u32[]{:S(2)}) copy-start(f32[1,16]{1,0:T(1,128)} %hw.1) | copy-start | bytes 196
  0.7 140.9 %copy-start = (f32[1,16]{1,0:T(1,128)S(1)}, f32[1,16]{1,0:T(1,128)}, u32[]{:S(2)}) copy-start(f32[1,16]{1,0:T(1,128)} %ha.1) | copy-start | bytes 196
